TPU v7x, 128 devices: a whole 4x4x4 slice. The times are simulated.
128 devices in a mesh: tp: 2 (over core), dpcp: 64 (over z, y, x).
Axes of the slice: x: 4, y: 4, z: 4, core: 2. Of those that a mesh axis runs over, the one named last changes fastest.
Arguments:
- hidden: bfloat16 [128, 512, 576], P('dpcp')
- labels: int32 [128, 512], P('dpcp')
- loss_mask: int32 [128, 512], P('dpcp')
- norm_gain: bfloat16 [576], replicated
- embedding: bfloat16 [49152, 576], P('tp')
Outputs:
- output 1: float32 [], replicated
- output 2: bfloat16 [128, 512, 576], P('dpcp')
- output 3: float32 [49152, 576], P('tp')
All inputs are finite; a program needn't handle non-finite values.
Results may differ from a plain program's by a relative error of at most 0.001.
Values sent between devices are 32-bit elements.
A program may use at most 1 GiB of HBM per device.

v0:
```python
import jax
import jax.numpy as jnp
from jax import lax
from jax.sharding import PartitionSpec as P

EPS = 1e-5


def norm_f32(hidden_blk, norm_gain):
    h_f32 = hidden_blk.astype(jnp.float32)
    inv_rms = lax.rsqrt(jnp.mean(h_f32 * h_f32, axis=-1, keepdims=True) + EPS)
    return h_f32 * inv_rms * norm_gain.astype(jnp.float32)


def solution(mesh):
    def local_body(hidden, labels, loss_mask, norm_gain, embedding):
        num_rows, seq_len, hidden_dim = hidden.shape
        tokens = num_rows * seq_len
        shard_rows = embedding.shape[0]
        hid_flat = hidden.reshape(tokens, hidden_dim)
        local_labels = labels.reshape(tokens) - lax.axis_index("tp") * shard_rows
        tok_mask = loss_mask.reshape(tokens).astype(jnp.float32)
        mask_count = lax.psum(jnp.sum(tok_mask), "dpcp")
        normed_f32, norm_back = jax.vjp(lambda h_in: norm_f32(h_in, norm_gain), hid_flat)
        normed = normed_f32.astype(jnp.bfloat16)
        logits = lax.dot_general(normed, embedding, (((1,), (1,)), ((), ())), preferred_element_type=jnp.float32)
        row_max = lax.pmax(jnp.max(logits, axis=-1), "tp")
        exp_vals = jnp.exp(logits - row_max[:, None])
        is_label = local_labels[:, None] == jnp.arange(shard_rows, dtype=jnp.int32)[None, :]
        part_stats = jnp.stack([jnp.sum(exp_vals, axis=-1), jnp.sum(jnp.where(is_label, logits, 0.0), axis=-1)])
        full_stats = lax.psum(part_stats, "tp")
        sum_exp = full_stats[0]
        lab_logit = full_stats[1]
        tok_loss = row_max + jnp.log(sum_exp) - lab_logit
        total_loss = lax.psum(jnp.sum(tok_mask * tok_loss), "dpcp") / mask_count
        prob_vals = exp_vals / sum_exp[:, None]
        d_logits = (jnp.where(is_label, prob_vals - 1.0, prob_vals) * (tok_mask / mask_count)[:, None]).astype(jnp.bfloat16)
        d_normed = lax.psum(jnp.dot(d_logits, embedding, preferred_element_type=jnp.float32), "tp")
        d_hidden = norm_back(d_normed)[0]
        grad_part = lax.dot_general(d_logits, normed, (((0,), (0,)), ((), ())), preferred_element_type=jnp.float32)
        grad_embed = lax.psum(grad_part, "dpcp")
        return total_loss, d_hidden.reshape(num_rows, seq_len, hidden_dim), grad_embed

    return jax.shard_map(
        local_body,
        mesh=mesh,
        in_specs=(P("dpcp", None, None), P("dpcp", None), P("dpcp", None), P(None), P("tp", None)),
        out_specs=(P(), P("dpcp", None, None), P("tp", None)),
        check_vma=False,
    )
```

profile of v0, /device:TPU:0, one launch (start us, length us, event | category | flops | bytes accessed | tf_op | source)
XLA Modules:
  0.0 951.0 jit_solution(8321370379324572649)
XLA Ops:
  7.2 1.5 fusion.3
  8.8 3.0 convert_bitcast_fusion
  11.9 0.5 copy-done.7
  12.4 1.9 copy.11
  14.4 1.4 copy-done
  15.8 0.2 multiply_convert_fusion.2.clone.4
  16.1 52.3 %fusion.8 = (f32[1024]{0:T(1024)S(1)}, f32[1024,24576]{1,0:T(8,128)}) fusion(bf16[24576,576]{0,1:T(8,128)(2,1)} %param.9, bf16[1024,576]{0,1:T(8,128)(2,1)S(1)} %multiply_convert_fusion.2.clone.4), kind=kOutput, calls=%fused_computation.26 | convolution fusion | flops 29016195072 | bytes 130158592 | tf_op jit(solution)/shard_map/dot_general | solution.py:26
  68.4 2.4 pmax.7
  70.8 36.6 %fusion.2 = (f32[1024]{0:T(1024)S(1)}, f32[1024]{0:T(1024)S(1)}) fusion(f32[1024,24576]{1,0:T(8,128)} %get-tuple-element.13, f32[1024]{0:T(1024)S(1)} %pmax.7, s32[1024]{0:T(1024)S(1)} %bitcast.34), kind=kLoop, calls=%fused_computation.6 | loop fusion | flops 125827072 | bytes 100679680 | tf_op jit(solution)/shard_map/reduce_sum | solution.py:30
  107.5 2.5 psum.35
  110.0 0.6 multiply_reduce_fusion.1
  110.6 0.7 convert_reduce_fusion
  111.2 181.4 %all-reduce = (f32[]{:T(128)}, f32[]{:T(128)}) all-reduce(f32[]{:T(128)} %multiply_reduce_fusion.1, f32[]{:T(128)} %convert_reduce_fusion), channel_id=1, replica_groups=mesh['tp'=2,'dpcp'=64] {'dpcp'}, use_global_device_ids=true, to_apply=%region_7.8 | all-reduce | flops 2 | bytes 16 | tf_op jit(solution)/shard_map/psum | solution.py:35
  292.6 0.6 broadcast_divide_fusion
  293.3 49.3 %fusion.1 = bf16[1024,24576]{1,0:T(8,128)(2,1)} fusion(f32[1024,24576]{1,0:T(8,128)} %get-tuple-element.13, f32[1024]{0:T(1024)S(1)} %broadcast_divide_fusion, f32[1024]{0:T(1024)S(1)} %bitcast.33, s32[1024]{0:T(1024)S(1)} %bitcast.35, f32[1024]{0:T(1024)S(1)} %pmax.7), kind=kLoop, calls=%fused_computation.2 | loop fusion | flops 176160768 | bytes 151011328 | tf_op jit(solution)/shard_map/convert_element_type | solution.py:37
  342.6 38.0 %fusion.9 = f32[1024,576]{0,1:T(8,128)} fusion(bf16[1024,24576]{1,0:T(8,128)(2,1)} %fusion.1, bf16[24576,576]{0,1:T(8,128)(2,1)} %param.9), kind=kOutput, calls=%fused_computation.27 | convolution fusion | flops 28991029248 | bytes 81002496 | tf_op jit(solution)/shard_map/dot_general | solution.py:38
  380.6 0.3 all-reduce.6.cloned.1.call-start
  380.9 1.4 copy-done.1
  382.3 45.0 %fusion.5 = f32[24576,576]{0,1:T(8,128)} fusion(bf16[1024,24576]{1,0:T(8,128)(2,1)} %fusion.1, f32[1024,576]{0,1:T(8,128)S(1)} %bitcast.27, f32[576]{0:T(1024)S(1)} %copy-done.4, f32[1024]{0:T(1024)S(1)} %copy-done.6), kind=kOutput, calls=%fused_computation.23 | convolution fusion | flops 28992798720 | bytes 109320448 | tf_op jit(solution)/shard_map/dot_general | solution.py:40
  428.7 2.1 multiply_reduce_fusion
  431.1 0.5 fusion.4
  431.6 1.1 copy.16
  432.7 471.8 %all-reduce.6.cloned.1.call-done = f32[24576,576]{0,1:T(8,128)} async-done(((f32[24576,576]{0,1:T(8,128)}), f32[24576,576]{0,1:T(8,128)}) %all-reduce.6.cloned.1.call-update) | async-done | bytes 56623120 | tf_op jit(solution)/shard_map/psum | solution.py:41
  904.4 38.6 %copy.19 = f32[24576,576]{0,1:T(8,128)} copy(f32[24576,576]{0,1:T(8,128)} %all-reduce.6.cloned.1.call-done) | data formatting | bytes 113246208
  (36 shorter events, 0.4 us)
Async XLA Ops:
  7.2 421.5 %all-reduce.4.cloned.1.call-start = ((), (), s32[]{:S(2)}) async-start(), calls=%async_computation | async-start | bytes 4718592 | tf_op jit(solution)/shard_map/psum | solution.py:38
  7.2 4.6 copy-start.10
  7.2 4.6 copy-start.11
  7.2 4.6 copy-start.9
  11.8 2.6 copy-start.3
  11.9 0.6 copy-start.7
  11.9 2.5 copy-start.5
  14.4 1.4 copy-start
  342.6 38.3 %copy-start.4 = (f32[576]{0:T(1024)S(1)}, f32[576]{0:T(1024)}, u32[]{:S(2)}) copy-start(f32[576]{0:T(1024)} %copy-done.3) | copy-start | bytes 6916
  342.6 38.3 %copy-start.6 = (f32[1024]{0:T(1024)S(1)}, f32[1024]{0:T(1024)}, u32[]{:S(2)}) copy-start(f32[1024]{0:T(1024)} %copy-done.5) | copy-start | bytes 12292
  380.6 1.7 copy-start.1
  380.6 523.8 %all-reduce.6.cloned.1.call-start = ((), (), s32[]{:S(2)}) async-start(), calls=%async_computation.1 | async-start | bytes 113246208 | tf_op jit(solution)/shard_map/psum | solution.py:41
  428.7 2.2 copy-start.8
  428.7 2.4 copy-start.2
Sparse Core Ops, SparseCore 0:
  380.8 19.8 all-reduce.3
  427.5 476.9 all-reduce.5
where the time goes:
time: 951 us
  waiting for transfers between devices  472 us (50%)
  blocking collectives  186 us (20%)
  matrix products  135 us (14%)
  other arithmetic  95.2 us (10%)
  local copies, waits for them, and re-layouts  45.1 us (5%)
  between operations  16.7 us (2%)
    psum x1, waiting for transfers between devices, local_body(): grad_embed = lax.psum(grad_part, 'dpcp')  472 us
    psum x1, blocking collectives, local_body(): total_loss = lax.psum(jnp.sum(tok_mask * tok_loss), 'dpcp') / mask_count  181 us
    dot_general x1, matrix products, local_body(): lax.dot_general(normed, embedding, (((1,), (1,)), ((), ())), preferred_el...  52.3 us
    convert_element_type x1, other arithmetic, local_body(): (jnp.where(is_label, prob_vals - 1.0, prob_vals) * (tok_mask / mask_count...  49.3 us
    dot_general x1, matrix products, local_body(): lax.dot_general(d_logits, normed, (((0,), (0,)), ((), ())), preferred_ele...  45 us
    unnamed x28, local copies, waits for them, and re-layouts  42.1 us
    dot_general x1, matrix products, local_body(): jnp.dot(d_logits, embedding, preferred_element_type=jnp.float32)  38 us
    reduce_sum x1, other arithmetic, local_body(): jnp.sum(exp_vals, axis=-1)  36.6 us
  transfers between devices with their start and end apart: 2, of which 1 were waited for; matrix products, arithmetic and copies ran while one was open for 5% of the time, Pallas kernels for 0%

commit v1 on v0

v1 whole, which is shorter than its diff:
```python
import functools

import jax
import jax.numpy as jnp
from jax import lax
from jax.experimental import pallas as pl
from jax.experimental.pallas import tpu as pltpu
from jax.sharding import Mesh
from jax.sharding import PartitionSpec as P

EPS = 1e-5
D = 576
T = 1024
HALF = 512
VSH = 24576
GZ = 4
VZ = VSH // GZ
CHUNKS = (1024, 2048, 2048, 1024)
LANES = 128
NEG = -3.0e38


def dot(a, b):
    return lax.dot_general(a, b, (((1,), (0,)), ((), ())), preferred_element_type=jnp.float32)


def dot_nt(a, b):
    return lax.dot_general(a, b, (((1,), (1,)), ((), ())), preferred_element_type=jnp.float32)


def params(**kw):
    return pltpu.CompilerParams(vmem_limit_bytes=62 * 1024 * 1024, **kw)


def cost(flops, nbytes, trans=0):
    return pl.CostEstimate(flops=int(flops), bytes_accessed=int(nbytes), transcendentals=int(trans))


def norm_kernel(h_ref, g_ref, u_ref, pay_ref):
    h = h_ref[0].astype(jnp.float32)
    inv = lax.rsqrt(jnp.sum(h * h, axis=0, keepdims=True) * (1.0 / D) + EPS)
    n = h * inv * g_ref[...]

    @pl.when(pl.program_id(0) == lax.axis_index("tp"))
    def _():
        pay_ref[...] = n

    u_ref[...] = n.T.astype(jnp.bfloat16)


def norm_call(hid_t, gain):
    return pl.pallas_call(
        norm_kernel,
        grid=(2,),
        in_specs=[
            pl.BlockSpec((1, D, HALF), lambda s: (s, 0, 0)),
            pl.BlockSpec((D, 1), lambda s: (0, 0)),
        ],
        out_specs=[
            pl.BlockSpec((HALF, D), lambda s: (s, 0)),
            pl.BlockSpec((D, HALF), lambda s: (0, 0)),
        ],
        out_shape=[
            jax.ShapeDtypeStruct((T, D), jnp.bfloat16),
            jax.ShapeDtypeStruct((D, HALF), jnp.float32),
        ],
        compiler_params=params(),
        name="norm",
    )(hid_t, gain)


def pack_kernel(own_ref, sib_ref, u_ref, ut_ref):
    me = lax.axis_index("tp")
    for src, half in ((own_ref, me), (sib_ref, 1 - me)):
        n = src[0]
        at = pl.ds(pl.multiple_of(half * HALF, HALF), HALF)
        ut_ref[:, at] = n.astype(jnp.bfloat16)
        u_ref[at, :] = n.T.astype(jnp.bfloat16)


def pack_call(own, sib):
    return pl.pallas_call(
        pack_kernel,
        grid=(GZ,),
        in_specs=[pl.BlockSpec((1, D, HALF), lambda z: (z, 0, 0))] * 2,
        out_specs=[
            pl.BlockSpec((T, D), lambda z: (z, 0)),
            pl.BlockSpec((D, T), lambda z: (0, z)),
        ],
        out_shape=[
            jax.ShapeDtypeStruct((GZ * T, D), jnp.bfloat16),
            jax.ShapeDtypeStruct((D, GZ * T), jnp.bfloat16),
        ],
        compiler_params=params(),
        name="pack",
    )(own, sib)


SVB = 2048
SSUB = 512
SPLIT = 9


def stats_kernel(last, m_in, s_in, u_ref, e_ref, out_ref, s_out, z_scr, m_scr, s_scr):
    @pl.when(pl.program_id(0) == 0)
    def _():
        if last:
            m_scr[...] = m_in[...]
            s_scr[...] = s_in[...]
        else:
            m_scr[...] = jnp.full_like(m_scr, NEG)
            s_scr[...] = jnp.zeros_like(s_scr)

    nsub = SVB // SSUB

    def fold(k):
        for r in range(0, T, 32):
            rows = slice(r, r + 32)
            parts = [z_scr[k, rows, j : j + LANES] for j in range(0, SSUB, LANES)]
            top = functools.reduce(jnp.maximum, parts)
            old = m_scr[rows, :]
            new = jnp.maximum(old, top)
            total = s_scr[rows, :] * jnp.exp(old - new)
            for p in parts:
                total = total + jnp.exp(p - new)
            m_scr[rows, :] = new
            s_scr[rows, :] = total

    for k in range(nsub):
        z_scr[k] = dot(u_ref[...], e_ref[:, k * SSUB : (k + 1) * SSUB])
        if k:
            fold(k - 1)
    fold(nsub - 1)

    @pl.when(pl.program_id(0) == pl.num_programs(0) - 1)
    def _():
        if not last:
            out_ref[...] = m_scr[...]
            s_out[...] = s_scr[...]
            return
        m_lane = m_scr[...]
        m_row = jnp.max(m_lane, axis=1, keepdims=True)
        s_row = jnp.sum(s_scr[...] * jnp.exp(m_lane - m_row), axis=1, keepdims=True)
        out_ref[...] = jnp.broadcast_to(m_row, (T, LANES)).T[0:8, :]
        s_out[...] = jnp.broadcast_to(s_row, (T, LANES)).T[0:8, :]


def stats_call(u, emb_t, before=None):
    total = VSH // SVB
    last = before is not None
    steps, start = (total - SPLIT, SPLIT) if last else (SPLIT, 0)
    shape = (8, T) if last else (T, LANES)
    carried = list(before) if last else []
    kernel = functools.partial(stats_kernel, last)
    if not last:
        kernel = functools.partial(kernel, None, None)
    return pl.pallas_call(
        kernel,
        grid=(steps,),
        in_specs=[pl.BlockSpec((T, LANES), lambda v: (0, 0))] * len(carried)
        + [
            pl.BlockSpec((T, D), lambda v: (0, 0)),
            pl.BlockSpec((D, SVB), lambda v: (0, v + start)),
        ],
        out_specs=[pl.BlockSpec(shape, lambda v: (0, 0))] * 2,
        out_shape=[jax.ShapeDtypeStruct(shape, jnp.float32)] * 2,
        scratch_shapes=[
            pltpu.VMEM((SVB // SSUB, T, SSUB), jnp.float32),
            pltpu.VMEM((T, LANES), jnp.float32),
            pltpu.VMEM((T, LANES), jnp.float32),
        ],
        compiler_params=params(),
        cost_estimate=cost(2 * T * D * SVB * steps, D * SVB * steps * 2, T * SVB * steps),
        name="stats_b" if last else "stats_a",
    )(*carried, u, emb_t)


def spread(row):
    return jnp.broadcast_to(row, (LANES, row.shape[1])).T


def delta_rows(z, row_max, inv_sum, weight, label, ids):
    p = jnp.exp(z - row_max) * inv_sum
    hit = label == ids
    return jnp.where(hit, p - 1.0, p) * weight, hit


def grad_kernel(vb, off, rows_ref, u_ref, ut_ref, e_ref, out_ref, st_scr, z_scr, d_scr):
    xb = pl.program_id(0)

    @pl.when(xb == 0)
    def _():
        for z in range(GZ):
            for k in range(4):
                st_scr[k, z * T : (z + 1) * T, :] = spread(rows_ref[z, k : k + 1, :])

    base = lax.axis_index("tp") * VSH + lax.axis_index("z") * VZ + off + xb * vb
    ids0 = lax.broadcasted_iota(jnp.int32, (32, LANES), 1) + base

    def logits(k, t0):
        z_scr[k] = dot(u_ref[pl.ds(t0, HALF), :], e_ref[...])

    def deltas(k, t0):
        for r in range(0, HALF, 32):
            at = pl.ds(t0 + r, 32)
            row_max, inv_sum, weight, label = (st_scr[i, at, :] for i in range(4))
            for j in range(0, vb, LANES):
                ids = (ids0 + j).astype(jnp.float32)
                d, _ = delta_rows(z_scr[k, r : r + 32, j : j + LANES], row_max, inv_sum, weight, label, ids)
                d_scr[k, r : r + 32, j : j + LANES] = d.astype(jnp.bfloat16)

    out_ref[...] = jnp.zeros_like(out_ref)

    @pl.loop(0, GZ)
    def _(i):
        ta = pl.multiple_of(i * T, T)
        tb = pl.multiple_of(i * T + HALF, HALF)
        logits(0, ta)
        logits(1, tb)
        deltas(0, ta)
        out_ref[:, 0] += dot(ut_ref[:, pl.ds(ta, HALF)], d_scr[0]).reshape(4, D // 4, vb)
        deltas(1, tb)
        out_ref[:, 0] += dot(ut_ref[:, pl.ds(tb, HALF)], d_scr[1]).reshape(4, D // 4, vb)


def grad_call(width, off, rows, u_all, ut_all, emb_t):
    vb = width // 4
    return pl.pallas_call(
        functools.partial(grad_kernel, vb, off),
        grid=(4,),
        in_specs=[
            pl.BlockSpec((GZ, 4, T), lambda x: (0, 0, 0)),
            pl.BlockSpec((GZ * T, D), lambda x: (0, 0), pipeline_mode=pl.Buffered(1)),
            pl.BlockSpec((D, GZ * T), lambda x: (0, 0), pipeline_mode=pl.Buffered(1)),
            pl.BlockSpec((D, vb), lambda x: (0, lax.axis_index("z") * (VZ // vb) + off // vb + x)),
        ],
        out_specs=pl.BlockSpec((4, 1, D // 4, vb), lambda x: (0, x, 0, 0)),
        out_shape=jax.ShapeDtypeStruct((4, 4, D // 4, vb), jnp.float32),
        scratch_shapes=[
            pltpu.VMEM((4, GZ * T, LANES), jnp.float32),
            pltpu.VMEM((2, HALF, vb), jnp.float32),
            pltpu.VMEM((2, HALF, vb), jnp.bfloat16),
        ],
        compiler_params=params(),
        cost_estimate=cost(4 * GZ * T * D * width, D * width * 6 + 4 * GZ * T * D, GZ * T * width),
        name=f"grad{off}",
    )(rows, u_all, ut_all, emb_t)


DVB = 1024
DSUB = 512


def du_kernel(rows_ref, u_ref, e_ref, du_ref, lab_ref, st_scr, z_scr, d_scr, l_scr):
    step = pl.program_id(0)

    @pl.when(step == 0)
    def _():
        for k in range(4):
            st_scr[k] = spread(rows_ref[k : k + 1, :])
        du_ref[...] = jnp.zeros_like(du_ref)
        l_scr[...] = jnp.zeros_like(l_scr)

    base = lax.axis_index("tp") * VSH + step * DVB
    ids0 = lax.broadcasted_iota(jnp.int32, (32, LANES), 1) + base

    def logits(k):
        z_scr[k] = dot(u_ref[...], e_ref[:, k * DSUB : (k + 1) * DSUB])

    def deltas(k):
        for r in range(0, T, 32):
            rows = slice(r, r + 32)
            row_max, inv_sum, weight, label = (st_scr[i, rows, :] for i in range(4))
            found = l_scr[rows, :]
            for j in range(0, DSUB, LANES):
                ids = (ids0 + (k * DSUB + j)).astype(jnp.float32)
                z = z_scr[k, rows, j : j + LANES]
                d, hit = delta_rows(z, row_max, inv_sum, weight, label, ids)
                found = found + jnp.where(hit, z, 0.0)
                d_scr[k, rows, j : j + LANES] = d.astype(jnp.bfloat16)
            l_scr[rows, :] = found

    def product(k):
        du_ref[...] += dot_nt(d_scr[k], e_ref[:, k * DSUB : (k + 1) * DSUB])

    logits(0)
    logits(1)
    deltas(0)
    product(0)
    deltas(1)
    product(1)

    @pl.when(step == pl.num_programs(0) - 1)
    def _():
        lab = jnp.sum(l_scr[...], axis=1, keepdims=True)
        lab_ref[...] = jnp.broadcast_to(lab, (T, LANES)).T[0:8, :]


def du_call(rows, u, emb_t):
    return pl.pallas_call(
        du_kernel,
        grid=(VSH // DVB,),
        in_specs=[
            pl.BlockSpec((4, T), lambda v: (0, 0)),
            pl.BlockSpec((T, D), lambda v: (0, 0)),
            pl.BlockSpec((D, DVB), lambda v: (0, v)),
        ],
        out_specs=[
            pl.BlockSpec((T, D), lambda v: (0, 0)),
            pl.BlockSpec((8, T), lambda v: (0, 0)),
        ],
        out_shape=[
            jax.ShapeDtypeStruct((T, D), jnp.float32),
            jax.ShapeDtypeStruct((8, T), jnp.float32),
        ],
        scratch_shapes=[
            pltpu.VMEM((4, T, LANES), jnp.float32),
            pltpu.VMEM((2, T, DSUB), jnp.float32),
            pltpu.VMEM((2, T, DSUB), jnp.bfloat16),
            pltpu.VMEM((T, LANES), jnp.float32),
        ],
        compiler_params=params(),
        cost_estimate=cost(4 * T * D * VSH, D * VSH * 2, T * VSH),
        name="du",
    )(rows, u, emb_t)


def place_kernel(g_ref, *rest):
    rest[-1][...] = g_ref[0, :, 0].reshape(D, g_ref.shape[-1])


def place_call(width, off, gathered, buf):
    vb = width // 4
    args, specs, alias = [gathered], [], {}
    specs.append(pl.BlockSpec((1, 4, 1, D // 4, vb), lambda z, x: (z, 0, x, 0, 0)))
    if buf is not None:
        args.append(buf)
        specs.append(pl.BlockSpec(memory_space=pl.ANY))
        alias = {1: 0}
    return pl.pallas_call(
        place_kernel,
        grid=(GZ, 4),
        in_specs=specs,
        out_specs=pl.BlockSpec((D, vb), lambda z, x: (0, z * (VZ // vb) + off // vb + x)),
        out_shape=jax.ShapeDtypeStruct((D, VSH), jnp.float32),
        input_output_aliases=alias,
        compiler_params=params(),
        cost_estimate=cost(D * width * 4, D * width * 32),
        name=f"place{off}",
    )(*args)


def norm_f32(hidden_blk, norm_gain):
    h_f32 = hidden_blk.astype(jnp.float32)
    inv_rms = lax.rsqrt(jnp.mean(h_f32 * h_f32, axis=-1, keepdims=True) + EPS)
    return h_f32 * inv_rms * norm_gain.astype(jnp.float32)


def solution(mesh):
    grid_mesh = Mesh(mesh.devices.reshape(2, 4, 4, 4), ("tp", "z", "y", "x"))
    swap = [(0, 1), (1, 0)]

    def local_body(hidden, labels, loss_mask, norm_gain, embedding):
        emb_t = embedding.T
        gain = norm_gain.astype(jnp.float32)[:, None]
        tok_mask = loss_mask.reshape(T).astype(jnp.float32)
        lab = labels.reshape(T).astype(jnp.float32)
        count = lax.psum(jnp.sum(tok_mask), ("tp", "z", "y", "x")) * 0.5
        weight = tok_mask / count

        u, pay = norm_call(hidden.transpose(0, 2, 1), gain)
        own = lax.all_gather(pay, "z", axis=0)
        lanes = stats_call(u, emb_t)
        own, _ = lax.optimization_barrier((own, lanes[0]))
        sib = lax.ppermute(own, "tp", swap)
        m_rows, s_rows = stats_call(u, emb_t, lanes)
        m_loc, s_loc = m_rows[0], s_rows[0]
        row_max = lax.pmax(m_loc, "tp")
        sum_exp = lax.psum(s_loc * jnp.exp(m_loc - row_max), "tp")
        rows = jnp.stack([row_max, 1.0 / sum_exp, weight, lab])
        rows_z = lax.all_gather(rows, "z", axis=0)

        u_all, ut_all = pack_call(own, sib)
        buf = None
        off = 0
        gathered = []
        for width in CHUNKS:
            part = grad_call(width, off, rows_z, u_all, ut_all, emb_t)
            mine = lax.psum_scatter(part.reshape(16, D // 4, width // 4), ("y", "x"), scatter_dimension=0)
            full = lax.all_gather(mine, ("z", "y", "x"), axis=0)
            gathered.append((width, off, full.reshape(GZ, 4, 4, D // 4, width // 4)))
            off += width

        du_part, lab_part = du_call(rows, u, emb_t)
        du = (du_part + lax.ppermute(du_part, "tp", swap)).reshape(2, HALF, D)
        _, norm_back = jax.vjp(lambda h_in: norm_f32(h_in, norm_gain), hidden)
        d_hidden = norm_back(du)[0]

        logs = jnp.where(lax.axis_index("tp") == 0, row_max + jnp.log(sum_exp), 0.0)
        loss = lax.psum(jnp.sum(tok_mask * (logs - lab_part[0])), ("tp", "z", "y", "x")) / count

        for width, off, full in gathered:
            buf = place_call(width, off, full, buf)
        return loss, d_hidden, buf.T

    dp = ("z", "y", "x")
    return jax.shard_map(
        local_body,
        mesh=grid_mesh,
        in_specs=(P(dp, None, None), P(dp, None), P(dp, None), P(None), P("tp", None)),
        out_specs=(P(), P(dp, None, None), P("tp", None)),
        check_vma=False,
    )
```

time: 951 us -> 932 us (0.980)
  Pallas kernels: 0 us -> 365 us
  matrix products: 135 us -> 0 us
  waiting for transfers between devices: 472 us -> 377 us
  other arithmetic: 95.2 us -> 7.44 us
  blocking collectives: 186 us -> 149 us
  local copies, waits for them, and re-layouts: 45.1 us -> 12.6 us
    psum x2 -> x0, waiting for transfers between devices: 472 us -> none  [the longest x1 472 us: local_body(): grad_embed = lax.psum(grad_part, 'dpcp')]
    pallas_call x0 -> x13, Pallas kernels: none -> 365 us  [the longest x4 129 us: grad_call(): pl.pallas_call(functools.partial(grad_kernel, vb, off), grid=(4,), in_spe...]
    unnamed x2 -> x13, waiting for transfers between devices: 0.03 us -> 211 us
    all_gather x0 -> x5, waiting for transfers between devices: none -> 166 us  [the longest x4 150 us: local_body(): full = lax.all_gather(mine, ('z', 'y', 'x'), axis=0)]
    dot_general x3 -> x0, matrix products: 135 us -> none  [the longest x1 52.3 us: local_body(): lax.dot_general(normed, embedding, (((1,), (1,)), ((), ())), preferred_el...]
    convert_element_type x2 -> x1, other arithmetic: 49.3 us -> 0.01 us  [local_body(): gain = norm_gain.astype(jnp.float32)[:, None]]
    psum x2 -> x3, blocking collectives: 184 us -> 135 us  [the longest x1 67.5 us: local_body(): lax.psum(jnp.sum(tok_mask * (logs - lab_part[0])), ('tp', 'z', 'y', 'x'))]
    unnamed x28 -> x13, local copies, waits for them, and re-layouts: 42.1 us -> 0.04 us
  transfers between devices with their start and end apart: 2 -> 11, of which waited for: 1 -> 6; matrix products, arithmetic and copies ran while one was open for 5% -> 2% of each run, Pallas kernels for 0% -> 34%
where the time goes in v1:
time: 932 us; the launch traced here: 929 us
  waiting for transfers between devices  377 us (40%)
  Pallas kernels  365 us (39%)
  blocking collectives  149 us (16%)
  between operations  16.4 us (2%)
  local copies, waits for them, and re-layouts  12.6 us (1%)
    unnamed x13, waiting for transfers between devices  211 us
    all_gather x4, waiting for transfers between devices, local_body(): full = lax.all_gather(mine, ('z', 'y', 'x'), axis=0)  150 us
    pallas_call x4, Pallas kernels, grad_call(): pl.pallas_call(functools.partial(grad_kernel, vb, off), grid=(4,), in_spe...  129 us
    pallas_call x1, Pallas kernels, du_call(): pl.pallas_call(du_kernel, grid=(VSH // DVB,), in_specs=[pl.BlockSpec((4,...  109 us
    psum x1, blocking collectives, local_body(): lax.psum(jnp.sum(tok_mask * (logs - lab_part[0])), ('tp', 'z', 'y', 'x'))  67.5 us
    psum x1, blocking collectives, local_body(): count = lax.psum(jnp.sum(tok_mask), ('tp', 'z', 'y', 'x')) * 0.5  65.2 us
    pallas_call x4, Pallas kernels, place_call(): pl.pallas_call(place_kernel, grid=(GZ, 4), in_specs=specs, out_specs=pl.B...  62.1 us
    pallas_call x2, Pallas kernels, stats_call(): pl.pallas_call(kernel, grid=(steps,), in_specs=[pl.BlockSpec((T, LANES),...  54.4 us
  transfers between devices with their start and end apart: 11, of which 6 were waited for; matrix products, arithmetic and copies ran while one was open for 2% of the time, Pallas kernels for 34%

profile of v1, /device:TPU:0, one launch (start us, length us, event | category | flops | bytes accessed | tf_op | source)
XLA Modules:
  0.0 929.3 jit_solution(16264327193373448492)
XLA Ops:
  12.0 38.8 %stats_a.1 = (f32[1024,128]{1,0:T(8,128)}, f32[1024,128]{1,0:T(8,128)}) custom-call(bf16[1024,576]{1,0:T(8,128)(2,1)} %get-tuple-element.14.u_ref, bf16[576,24576]{1,0:T(8,128)(2,1)} %bitcast.33), custom_call_target="tpu_custom_call" | custom-call | flops 21743271936 | bytes 21233664 | tf_op jit(solution)/shard_map/stats_a/pallas_call | solution.py:157
  50.8 16.4 %all-gather.17.cloned.1.call-done = f32[2304,512]{1,0:T(8,128)} async-done(((f32[576,512]{1,0:T(8,128)}), f32[2304,512]{1,0:T(8,128)}) %all-gather.17.cloned.1.call-update) | async-done | bytes 4718608 | tf_op jit(solution)/shard_map/all_gather | solution.py:372
  67.9 65.2 %psum.22 = f32[]{:T(128)} all-reduce(f32[]{:T(128)} %convert_reduce_fusion), channel_id=1, replica_groups=mesh['tp'=2,'z'=4,'y'=4,'x'=4] {'tp','z','y','x'}, use_global_device_ids=true, to_apply=%region_3.0 | all-reduce | flops 1 | bytes 8 | tf_op jit(solution)/shard_map/psum | solution.py:368
  133.1 15.5 %stats_b.1 = (f32[8,1024]{1,0:T(8,128)}, f32[8,1024]{1,0:T(8,128)}) custom-call(f32[1024,128]{1,0:T(8,128)} %get-tuple-element.15.m_in, f32[1024,128]{1,0:T(8,128)} %get-tuple-element.16.s_in, bf16[1024,576]{1,0:T(8,128)(2,1)} %get-tuple-element.14.u_ref, bf16[576,24576]{1,0:T(8,128)(2,1)} %bitcast.34), custom_call_target="tpu_custom_call" | custom-call | flops 7247757312 | bytes 7077888 | tf_op jit(solution)/shard_map/stats_b/pallas_call | solution.py:157
  156.4 11.9 %all-gather.2.rows_ref = f32[4,4,1024]{2,1,0:T(4,128)} all-gather(f32[1,4,1024]{2,1,0:T(4,128)S(1)} %get-tuple-element.27), channel_id=2, replica_groups=mesh['tp'=2,'z'=4,'y'=4,'x'=4] {'z'}, dimensions={0}, use_global_device_ids=true | all-gather | bytes 81920 | tf_op jit(solution)/shard_map/all_gather | solution.py:381
  168.3 8.0 pack.1
  176.3 26.4 %grad0.1 = f32[4,4,144,256]{3,2,1,0:T(8,128)} custom-call(f32[4,4,1024]{2,1,0:T(4,128)} %all-gather.2.rows_ref, bf16[4096,576]{1,0:T(8,128)(2,1)} %get-tuple-element.23.u_ref, bf16[576,4096]{1,0:T(8,128)(2,1)} %get-tuple-element.24.ut_ref, bf16[576,24576]{1,0:T(8,128)(2,1)} %bitcast.35), custom_call_target="tpu_custom_call" | custom-call | flops 9663676416 | bytes 12976128 | tf_op jit(solution)/shard_map/grad0/pallas_call | solution.py:228
  203.0 38.1 %grad1024.1 = f32[4,4,144,512]{3,2,1,0:T(8,128)} custom-call(f32[4,4,1024]{2,1,0:T(4,128)} %all-gather.2.rows_ref, bf16[4096,576]{1,0:T(8,128)(2,1)} %get-tuple-element.23.u_ref, bf16[576,4096]{1,0:T(8,128)(2,1)} %get-tuple-element.24.ut_ref, bf16[576,24576]{1,0:T(8,128)(2,1)} %bitcast.36), custom_call_target="tpu_custom_call" | custom-call | flops 19327352832 | bytes 16515072 | tf_op jit(solution)/shard_map/grad1024/pallas_call | solution.py:228
  241.1 38.1 %grad3072.1 = f32[4,4,144,512]{3,2,1,0:T(8,128)} custom-call(f32[4,4,1024]{2,1,0:T(4,128)} %all-gather.2.rows_ref, bf16[4096,576]{1,0:T(8,128)(2,1)} %get-tuple-element.23.u_ref, bf16[576,4096]{1,0:T(8,128)(2,1)} %get-tuple-element.24.ut_ref, bf16[576,24576]{1,0:T(8,128)(2,1)} %bitcast.37), custom_call_target="tpu_custom_call" | custom-call | flops 19327352832 | bytes 16515072 | tf_op jit(solution)/shard_map/grad3072/pallas_call | solution.py:228
  279.2 26.5 %grad5120.1 = f32[4,4,144,256]{3,2,1,0:T(8,128)} custom-call(f32[4,4,1024]{2,1,0:T(4,128)} %all-gather.2.rows_ref, bf16[4096,576]{1,0:T(8,128)(2,1)} %get-tuple-element.23.u_ref, bf16[576,4096]{1,0:T(8,128)(2,1)} %get-tuple-element.24.ut_ref, bf16[576,24576]{1,0:T(8,128)(2,1)} %bitcast.38), custom_call_target="tpu_custom_call" | custom-call | flops 9663676416 | bytes 12976128 | tf_op jit(solution)/shard_map/grad5120/pallas_call | solution.py:228
  306.4 51.3 %reduce-scatter.17.cloned.1.call-done = f32[1,144,512]{2,1,0:T(8,128)} async-done(((f32[16,144,512]{2,1,0:T(8,128)}), f32[1,144,512]{2,1,0:T(8,128)}) %reduce-scatter.17.cloned.1.call-update) | async-done | bytes 294928
  357.7 81.3 %reduce-scatter.15.cloned.1.call-done = f32[1,144,512]{2,1,0:T(8,128)} async-done(((f32[16,144,512]{2,1,0:T(8,128)}), f32[1,144,512]{2,1,0:T(8,128)}) %reduce-scatter.15.cloned.1.call-update) | async-done | bytes 294928
  439.3 77.6 %reduce-scatter.13.cloned.1.call-done = f32[1,144,256]{2,1,0:T(8,128)} async-done(((f32[16,144,256]{2,1,0:T(8,128)}), f32[1,144,256]{2,1,0:T(8,128)}) %reduce-scatter.13.cloned.1.call-update) | async-done | bytes 147472
  517.0 108.6 %du.1 = (f32[1024,576]{1,0:T(8,128)}, f32[8,1024]{1,0:T(8,128)}) custom-call(f32[4,1024]{1,0:T(4,128)} %get-tuple-element.28.rows_ref, bf16[1024,576]{1,0:T(8,128)(2,1)} %get-tuple-element.14.u_ref, bf16[576,24576]{1,0:T(8,128)(2,1)} %bitcast.39), custom_call_target="tpu_custom_call" | custom-call | flops 57982058496 | bytes 28311552 | tf_op jit(solution)/shard_map/du/pallas_call | solution.py:300
  625.6 3.2 copy.15
  630.1 67.5 %psum.23 = f32[]{:T(128)} all-reduce(f32[]{:T(128)} %multiply_reduce_fusion), channel_id=1, replica_groups=mesh['tp'=2,'z'=4,'y'=4,'x'=4] {'tp','z','y','x'}, use_global_device_ids=true, to_apply=%region_5.0 | all-reduce | flops 1 | bytes 8 | tf_op jit(solution)/shard_map/psum | solution.py:400
  698.3 3.4 copy.16
  701.7 3.5 add.34
  709.5 12.4 %place0.1.rest_0_ = f32[576,24576]{1,0:T(8,128)} custom-call(f32[4,4,4,144,256]{4,3,2,1,0:T(8,128)} %bitcast.46), custom_call_target="tpu_custom_call" | custom-call | flops 2359296 | bytes 18874368 | tf_op jit(solution)/shard_map/place0/pallas_call | solution.py:340
  721.9 18.7 %place1024.1.rest_0_ = f32[576,24576]{1,0:T(8,128)} custom-call(f32[4,4,4,144,512]{4,3,2,1,0:T(8,128)} %bitcast.40, f32[576,24576]{1,0:T(8,128)} %place0.1.rest_0_), custom_call_target="tpu_custom_call", output_to_operand_aliasing={{}: (1, {})} | custom-call | flops 4718592 | bytes 37748736 | tf_op jit(solution)/shard_map/place1024/pallas_call | solution.py:340
  740.6 85.1 %all-gather.11.cloned.1.call-done = f32[64,144,512]{2,1,0:T(8,128)} async-done(((f32[1,144,512]{2,1,0:T(8,128)}), f32[64,144,512]{2,1,0:T(8,128)}) %all-gather.11.cloned.1.call-update) | async-done | bytes 18874384 | tf_op jit(solution)/shard_map/all_gather | solution.py:390
  825.7 18.7 %place3072.1.rest_0_ = f32[576,24576]{1,0:T(8,128)} custom-call(f32[4,4,4,144,512]{4,3,2,1,0:T(8,128)} %bitcast.41, f32[576,24576]{1,0:T(8,128)} %place1024.1.rest_0_), custom_call_target="tpu_custom_call", output_to_operand_aliasing={{}: (1, {})} | custom-call | flops 4718592 | bytes 37748736 | tf_op jit(solution)/shard_map/place3072/pallas_call | solution.py:340
  844.4 64.9 %all-gather.9.cloned.1.call-done = f32[64,144,256]{2,1,0:T(8,128)} async-done(((f32[1,144,256]{2,1,0:T(8,128)}), f32[64,144,256]{2,1,0:T(8,128)}) %all-gather.9.cloned.1.call-update) | async-done | bytes 9437200 | tf_op jit(solution)/shard_map/all_gather | solution.py:390
  909.3 12.4 %place5120.1 = f32[576,24576]{1,0:T(8,128)} custom-call(f32[4,4,4,144,256]{4,3,2,1,0:T(8,128)} %bitcast.47, f32[576,24576]{1,0:T(8,128)} %place3072.1.rest_0_), custom_call_target="tpu_custom_call", output_to_operand_aliasing={{}: (1, {})} | custom-call | flops 2359296 | bytes 18874368 | tf_op jit(solution)/shard_map/place5120/pallas_call | solution.py:340
  (58 shorter events, 19.5 us)
Async XLA Ops:
  7.2 60.1 %all-gather.17.cloned.1.call-start = ((), (), s32[]{:S(2)}) async-start(), calls=%async_computation.8 | async-start | bytes 5898240 | tf_op jit(solution)/shard_map/all_gather | solution.py:372
  11.9 293.9 %reduce-scatter.19.cloned.1.call-start = ((), (), s32[]{:S(2)}) async-start(), calls=%async_computation.12 | async-start | bytes 2506752
  11.9 55.3 %copy-start.2 = (s32[2,512]{1,0:T(2,128)S(1)}, s32[2,512]{1,0:T(2,128)}, u32[]{:S(2)}) copy-start(s32[2,512]{1,0:T(2,128)} %param.7) | copy-start | bytes 12292
  67.2 101.0 %collective-permute-start.1 = (f32[4,576,512]{2,1,0:T(8,128)}, f32[4,576,512]{2,1,0:T(8,128)}, u32[]{:S(2)}, u32[]{:S(2)}) collective-permute-start(f32[4,576,512]{2,1,0:T(8,128)} %bitcast.48), channel_id=1, source_target_pairs={{0,64},{64,0},{1,65},{65,1},{2,66},{66,2},{3,67},{67,3},{4,68},{68... | collective-permute-start | bytes 14155784 | tf_op jit(solution)/shard_map/ppermute | solution.py:375
  133.1 17.8 %copy-start.4 = (s32[2,512]{1,0:T(2,128)S(1)}, s32[2,512]{1,0:T(2,128)}, u32[]{:S(2)}) copy-start(s32[2,512]{1,0:T(2,128)} %param.6) | copy-start | bytes 12292
  202.7 154.9 %reduce-scatter.17.cloned.1.call-start = ((), (), s32[]{:S(2)}) async-start(), calls=%async_computation.11 | async-start | bytes 5013504
  241.1 198.0 %reduce-scatter.15.cloned.1.call-start = ((), (), s32[]{:S(2)}) async-start(), calls=%async_computation.10 | async-start | bytes 5013504
  279.2 237.7 %reduce-scatter.13.cloned.1.call-start = ((), (), s32[]{:S(2)}) async-start(), calls=%async_computation.9 | async-start | bytes 2506752
  305.7 403.8 %all-gather.15.cloned.1.call-start = ((), (), s32[]{:S(2)}) async-start(), calls=%async_computation.7 | async-start | bytes 9584640 | tf_op jit(solution)/shard_map/all_gather | solution.py:390
  306.3 415.6 %all-gather.13.cloned.1.call-start = ((), (), s32[]{:S(2)}) async-start(), calls=%async_computation.6 | async-start | bytes 19169280 | tf_op jit(solution)/shard_map/all_gather | solution.py:390
  357.6 468.1 %all-gather.11.cloned.1.call-start = ((), (), s32[]{:S(2)}) async-start(), calls=%async_computation.5 | async-start | bytes 19169280 | tf_op jit(solution)/shard_map/all_gather | solution.py:390
  439.1 470.2 %all-gather.9.cloned.1.call-start = ((), (), s32[]{:S(2)}) async-start(), calls=%async_computation.4 | async-start | bytes 9584640 | tf_op jit(solution)/shard_map/all_gather | solution.py:390
  625.6 72.1 %copy-start.3 = (bf16[576]{0:T(1024)(128)(2,1)S(1)}, bf16[576]{0:T(1024)(128)(2,1)}, u32[]{:S(2)}) copy-start(bf16[576]{0:T(1024)(128)(2,1)} %param.8) | copy-start | bytes 3460
  628.8 69.6 %collective-permute-start = (f32[1024,576]{0,1:T(8,128)}, f32[1024,576]{0,1:T(8,128)}, u32[]{:S(2)}, u32[]{:S(2)}) collective-permute-start(f32[1024,576]{0,1:T(8,128)} %copy.15), channel_id=1, source_target_pairs={{0,64},{64,0},{1,65},{65,1},{2,66},{66,2},{3,67},{67,3},{4,68},{68... | collective-permute-start | bytes 7077896 | tf_op jit(solution)/shard_map/ppermute | solution.py:395
  698.3 3.4 copy-start.1
  705.2 2.2 copy-start
Sparse Core Ops, SparseCore 0:
  12.0 55.1 all-gather.16
  202.9 72.8 reduce-scatter.18
  279.1 78.4 reduce-scatter.16
  360.8 78.1 reduce-scatter.14
  442.2 74.7 reduce-scatter.12
  519.5 80.5 all-gather.14
  602.9 110.9 all-gather.12
  716.7 108.9 all-gather.10
  828.5 80.7 all-gather.8

commit v2 on v0

v2 whole, which is shorter than its diff:
```python
import functools

import jax
import jax.numpy as jnp
from jax import lax
from jax.experimental import pallas as pl
from jax.experimental.pallas import tpu as pltpu
from jax.sharding import Mesh
from jax.sharding import PartitionSpec as P

EPS = 1e-5
N = {"tp": 2, "z": 4, "y": 4, "x": 4}
D = 576
DP = 640
HALF = 512
T = 2 * HALF
VSH = 24576
VB = 128
SVB, DVB, SUB = 2048, 2048, 512
K = 12
NP = 4
YR = 144
RH = 72
LANES = 128
NEG = -3.0e38
COLORS = (("yzx", (24, 24)), ("xzy", (24, 24)), ("xyz", (24, 24)))
BOTH = ((0, 1), (1, 3))
F32, BF16 = jnp.float32, jnp.bfloat16
FAR = (1, 3, 2)
PAIR, TRIPLE = range(2), range(3)


def mean0(x):
    return jnp.sum(x, axis=0, keepdims=True) * (1.0 / D)


def fold1(op, x):
    return op(x, axis=1, keepdims=True)


def along(axis, *shape):
    return pl.BlockSpec(shape, lambda s: tuple(s if i == axis else 0 for i in range(len(shape))))


def dot(a, b):
    return lax.dot_general(a, b, (((1,), (0,)), ((), ())), preferred_element_type=F32)


def dot_nt(a, b):
    return lax.dot_general(a, b, (((1,), (1,)), ((), ())), preferred_element_type=F32)


def pos(axis, by=0):
    return lax.rem(lax.axis_index(axis) + by, N[axis])


def peers(axis):
    return FAR[: N[axis] - 1]


def whole(shape, **kw):
    return pl.BlockSpec(shape, lambda *_: (0,) * len(shape), **kw)


ANY = pl.BlockSpec(memory_space=pl.ANY)


def push(src, dst, send, recv, axis, by):
    pltpu.make_async_remote_copy(
        src_ref=src,
        dst_ref=dst,
        send_sem=send,
        recv_sem=recv,
        device_id={axis: pos(axis, by)},
        device_id_type=pl.DeviceIdType.MESH,
    ).start()


def wait(ref, sem):
    pltpu.make_async_copy(ref, ref, sem).wait()


def enter():
    barrier = pltpu.get_barrier_semaphore()
    count = 0
    for axis in N:
        for by in peers(axis):
            pl.semaphore_signal(
                barrier, inc=1, device_id={axis: pos(axis, by)}, device_id_type=pl.DeviceIdType.MESH
            )
            count += 1
    pl.semaphore_wait(barrier, count)


def total(step, axes, own, got, send, recv):
    if step > 0:
        acc = own[step - 1]
        for i, _ in enumerate(peers(axes[step - 1])):
            wait(got.at[step - 1, i], recv.at[step - 1, i])
            wait(got.at[step - 1, i], send.at[step - 1, i])
        for i, _ in enumerate(peers(axes[step - 1])):
            acc = acc + got[step - 1, i]
        own[step] = acc
    if step < len(axes):
        for i, by in enumerate(peers(axes[step])):
            push(own.at[step], got.at[step, i], send.at[step, i], recv.at[step, i], axes[step], by)


def params(**kw):
    return pltpu.CompilerParams(vmem_limit_bytes=63 << 20, **kw)


def cost(flops, nbytes):
    return pl.CostEstimate(flops=int(flops), bytes_accessed=int(nbytes), transcendentals=0)


def norm_kernel(h_ref, g_ref, u_ref, ut_ref, pay_ref):
    h = h_ref[0].astype(F32)
    inv = lax.rsqrt(mean0(h * h) + EPS)
    n = h * inv * g_ref[...]

    @pl.when(pl.program_id(0) == lax.axis_index("tp"))
    def _():
        pay_ref[...] = n

    ut_ref[...] = n.astype(BF16)
    u_ref[...] = n.T.astype(BF16)


def norm_call(hid_t, gain):
    return pl.pallas_call(
        norm_kernel,
        grid=(2,),
        in_specs=[along(0, 1, D, HALF), whole((D, 1))],
        out_specs=[
            along(0, HALF, D),
            along(1, D, HALF),
            whole((D, HALF)),
        ],
        out_shape=[
            jax.ShapeDtypeStruct((T, D), BF16),
            jax.ShapeDtypeStruct((D, T), BF16),
            jax.ShapeDtypeStruct((D, HALF), F32),
        ],
        compiler_params=params(),
        name="norm",
    )(hid_t, gain)


def norm_back_kernel(h_ref, g_ref, du_ref, out_ref):
    h = h_ref[0].astype(F32)
    inv = lax.rsqrt(mean0(h * h) + EPS)
    gdu = (du_ref[0] + du_ref[1]).T[:D] * g_ref[...]
    mean = mean0(h * gdu)
    out_ref[0] = (inv * gdu - h * (inv * inv * inv * mean)).astype(BF16)


def norm_back_call(hid_t, gain, du):
    block = along(0, 1, D, HALF)
    return pl.pallas_call(
        norm_back_kernel,
        grid=(2,),
        in_specs=[block, whole((D, 1)), along(1, 2, HALF, DP)],
        out_specs=block,
        out_shape=jax.ShapeDtypeStruct((2, D, HALF), BF16),
        compiler_params=params(),
        name="norm_back",
    )(hid_t, gain, du)


def stats_kernel(
    pay, mask_ref, lab_ref, u_ref, e_ref, z_ref, rows_ref, ug, m_scr, s_scr, own, got, ms, rows_got, *sems
):
    c_send, c_recv, u_send, u_recv, r_send, r_recv = sems
    step, steps = pl.program_id(0), pl.num_programs(0)
    cut = D // 2
    near = ((1, 0), (3, 1))

    def at(index, tick):
        pl.when(step == index)(tick)

    def begin():
        m_scr[...] = jnp.full_like(m_scr, NEG)
        s_scr[...] = jnp.zeros_like(s_scr)
        own[0] = jnp.broadcast_to(jnp.sum(mask_ref[...].astype(F32)), own.shape[1:])
        enter()
        if N["z"] > 1:
            for by, i in near:
                push(pay, ug.at[0, i], u_send.at[0, i], u_recv.at[0, i], "z", by)
        total(0, "xyz", own, got, c_send, c_recv)

    def pass_on():
        if N["z"] > 1:
            for i in PAIR:
                wait(ug.at[0, i], u_recv.at[0, i])
            for by, i in near:
                piece = pl.ds(i * cut, cut)
                push(ug.at[0, i, piece], ug.at[0, 2, piece], u_send.at[0, 2 + i], u_recv.at[0, 2 + i], "z", by)
                if N["tp"] > 1:
                    push(ug.at[0, i], ug.at[1, i], u_send.at[1, i], u_recv.at[1, i], "tp", 1)

    def share_far():
        if N["z"] > 1:
            for i in PAIR:
                wait(ug.at[0, 2, pl.ds(i * cut, cut)], u_recv.at[0, 2 + i])
            if N["tp"] > 1:
                push(ug.at[0, 2], ug.at[1, 2], u_send.at[1, 2], u_recv.at[1, 2], "tp", 1)

    at(0, begin)
    for i in range(1, 4):
        at(i, functools.partial(total, i, "xyz", own, got, c_send, c_recv))
    at(steps * 7 // 12, pass_on)
    at(steps - 1, share_far)

    def fold(k):
        for r in range(0, T, 64):
            rows = slice(r, r + 64)
            parts = [z_ref[rows, j : j + LANES] for j in range(k * SUB, (k + 1) * SUB, LANES)]
            old = m_scr[rows, :]
            new = functools.reduce(jnp.maximum, parts, old)
            acc = s_scr[rows, :] * jnp.exp(old - new)
            for p in parts:
                acc = acc + jnp.exp(p - new)
            m_scr[rows, :] = new
            s_scr[rows, :] = acc

    for k in range(SVB // SUB):
        z_ref[:, k * SUB : (k + 1) * SUB] = dot(u_ref[...], e_ref[:, k * SUB : (k + 1) * SUB])
        if k:
            fold(k - 1)
    fold(SVB // SUB - 1)

    @pl.when(step == steps - 1)
    def _():
        m_lane = m_scr[...]
        m_row = fold1(jnp.max, m_lane)
        s_row = fold1(jnp.sum, s_scr[...] * jnp.exp(m_lane - m_row))
        for i, row in enumerate((m_row, s_row)):
            ms[0, 8 * i : 8 * (i + 1)] = jnp.broadcast_to(row, (T, LANES)).T[:8]
        if N["tp"] > 1:
            push(ms.at[0], ms.at[1], r_send.at[3], r_recv.at[3], "tp", 1)
            wait(ms.at[1], r_recv.at[3])
            wait(ms.at[0], r_send.at[3])
        count = own[3, :1, :1]
        rows_ref[0, 4:8, :] = jnp.broadcast_to(1.0 / count, (4, T))
        swap = lax.axis_index("tp") == 1
        for k in PAIR:
            here = slice(k * HALF, (k + 1) * HALF)
            mask = mask_ref[k : k + 1, :].astype(F32)
            top, whole_sum = ms[0, :1, here], ms[0, 8:9, here]
            if N["tp"] > 1:
                m1, m2 = top, ms[1, :1, here]
                top = jnp.maximum(m1, m2)
                a, b = whole_sum * jnp.exp(m1 - top), ms[1, 8:9, here] * jnp.exp(m2 - top)
                whole_sum = jnp.where(swap, b + a, a + b)
            rows_ref[0, :1, here] = top
            rows_ref[0, 1:2, here] = mask / count / whole_sum
            rows_ref[0, 2:3, here] = jnp.where(mask > 0.0, lab_ref[k : k + 1, :].astype(F32), -1.0)
            rows_ref[0, 3:4, here] = mask * (top + jnp.log(whole_sum))
        rows_got[0] = rows_ref[0]
        for i, by in enumerate(peers("z")):
            push(rows_got.at[0], rows_got.at[1 + i], r_send.at[i], r_recv.at[i], "z", by)
        for i, _ in enumerate(peers("z")):
            wait(rows_got.at[1 + i], r_recv.at[i])
            wait(rows_got.at[0], r_send.at[i])
            rows_ref[1 + i] = rows_got[1 + i]
        if N["z"] > 1:
            for i in PAIR:
                wait(pay, u_send.at[0, i])
                wait(ug.at[0, 2, pl.ds(i * cut, cut)], u_send.at[0, 2 + i])
            if N["tp"] > 1:
                for i in TRIPLE:
                    wait(ug.at[0, i], u_send.at[1, i])
                    wait(ug.at[1, i], u_recv.at[1, i])


def stats_call(pay, mask, lab, u, emb_t):
    dma = pltpu.SemaphoreType.DMA
    return pl.pallas_call(
        stats_kernel,
        grid=(VSH // SVB,),
        in_specs=[
            ANY,
            whole((2, HALF)),
            whole((2, HALF)),
            whole((T, D)),
            along(1, D, SVB),
        ],
        out_specs=[along(1, T, SVB), whole((N["z"], 8, T)), ANY],
        out_shape=[
            jax.ShapeDtypeStruct((T, VSH), F32),
            jax.ShapeDtypeStruct((N["z"], 8, T), F32),
            jax.ShapeDtypeStruct((2, 3, D, HALF), F32),
        ],
        scratch_shapes=[
            pltpu.VMEM((T, LANES), F32),
            pltpu.VMEM((T, LANES), F32),
            pltpu.VMEM((4, 8, LANES), F32),
            pltpu.VMEM((3, 3, 8, LANES), F32),
            pltpu.VMEM((2, 16, T), F32),
            pltpu.VMEM((4, 8, T), F32),
            dma((3, 3)),
            dma((3, 3)),
            dma((2, 4)),
            dma((2, 4)),
            dma((4,)),
            dma((4,)),
        ],
        compiler_params=params(collective_id=1, has_side_effects=True),
        cost_estimate=cost(2 * T * D * VSH, T * VSH * 4),
        name="stats",
    )(pay, mask, lab, u, emb_t)


def pack_kernel(u_ref, ut_ref, own_ref, sib_ref, u_out, ut_out):
    r = pl.program_id(0)

    @pl.when(r == 0)
    def _():
        u_out[...] = u_ref[...]
        ut_out[...] = ut_ref[...]

    @pl.when(r > 0)
    def _():
        me = lax.axis_index("tp")
        for src, half in ((own_ref, me), (sib_ref, 1 - me)):
            n = src[0, 0]
            here = pl.ds(pl.multiple_of(half * HALF, HALF), HALF)
            ut_out[:, here] = n.astype(BF16)
            u_out[here, :] = n.T.astype(BF16)


def pack_call(u, ut, ug):
    piece = [pl.BlockSpec((1, 1, D, HALF), lambda r, c=c: (c, jnp.maximum(r - 1, 0), 0, 0)) for c in PAIR]
    return pl.pallas_call(
        pack_kernel,
        grid=(N["z"],),
        in_specs=[whole((T, D)), whole((D, T)), *piece],
        out_specs=[along(0, T, D), along(1, D, T)],
        out_shape=[
            jax.ShapeDtypeStruct((N["z"] * T, D), BF16),
            jax.ShapeDtypeStruct((D, N["z"] * T), BF16),
        ],
        compiler_params=params(),
        name="pack",
    )(u, ut, ug, ug)


def spread(row):
    return jnp.broadcast_to(row, (LANES, row.shape[1])).T


def main_kernel(rows_ref, u_ref, ut_ref, eg_ref, ed_ref, z_hbm, g, du, loss_ref, *scr):
    (st, zs, ds, p, ra1, ra2, rb1, rb2, sums, s_scr, zb, acc, dd, found, own, got) = scr[:16]
    rs_send, rs_recv, ag_send, ag_recv, l_send, l_recv, d_send, d_recv, local, z_sem = scr[16:]
    slot = pl.program_id(0)
    nx, ny = N["x"], N["y"]
    dus = VSH // DVB
    wg = nx * VB
    quarter = VSH // N["z"]
    parts = tuple(enumerate(("xy", "yx"))) if nx > 1 else ()
    cut = RH // 16 * 8


    def block(part, k, i, half=None):
        two = slice(None) if half is None else pl.ds(2 * half, 2)
        if part == 0:
            return p.at[lax.rem(k, NP), i, two, pl.ds(0, RH)]
        return p.at[lax.rem(k, NP), two, i, pl.ds(RH, RH)]

    def line(part, k, i, half=None):
        rows = (slice(None), pl.ds(0, cut), pl.ds(cut, RH - cut))[0 if half is None else 1 + half]
        return sums.at[lax.rem(k, NP), part, i, rows]

    def rs_push(k, part, stage, src, dst, axis, by):
        push(src, dst, rs_send.at[k, part], rs_recv.at[k, part, stage], axis, by)

    def rb1_at(k, part, half):
        return rb1.at[k, part, pl.ds(half * cut, RH - cut if half else cut)]

    def reduce_start(k):
        for part, (axis, _) in parts:
            for half, by in BOTH:
                rs_push(k, part, 0, block(part, k, pos(axis, 2), half), ra1.at[k, part, half], axis, by)

    def reduce_pass(k):
        for part, (axis, _) in parts:
            wait(ra1.at[k, part], rs_recv.at[k, part, 0])
            for half, by in BOTH:
                block(part, k, pos(axis, by), half)[...] += ra1[k, part, half]
        for part, (axis, _) in parts:
            for half, by in BOTH:
                rs_push(k, part, 1, block(part, k, pos(axis, by)), ra2.at[k, part, half], axis, by)

    def reduce_turn(k):
        for part, (axis, _) in parts:
            wait(ra2.at[k, part], rs_recv.at[k, part, 1])
            sums[lax.rem(k, NP), part] = block(part, k, pos(axis))[...] + ra2[k, part, 0] + ra2[k, part, 1]
        for part, (_, axis) in parts:
            for half, by in BOTH:
                rs_push(k, part, 2, line(part, k, pos(axis, 2), half), rb1_at(k, part, half), axis, by)

    def reduce_pass2(k):
        for part, (_, axis) in parts:
            wait(rb1.at[k, part], rs_recv.at[k, part, 2])
            for half, by in BOTH:
                line(part, k, pos(axis, by), half)[...] += rb1_at(k, part, half)[...]
        for part, (_, axis) in parts:
            for half, by in BOTH:
                rs_push(k, part, 3, line(part, k, pos(axis, by)), rb2.at[k, part, half], axis, by)

    def reduce_end(k):
        if not parts:
            s_scr[k] = p[lax.rem(k, NP), 0, 0]
        for part, (_, axis) in parts:
            wait(rb2.at[k, part], rs_recv.at[k, part, 3])
            s_scr[k, pl.ds(part * RH, RH)] = line(part, k, pos(axis))[...] + rb2[k, part, 0] + rb2[k, part, 1]
            wait(g.at[0, pl.ds(0, RH), pl.ds(0, 15 * VB)], rs_send.at[k, part])
        here = pl.ds(pl.multiple_of(pos("z") * quarter + k * wg + pos("x") * VB, LANES), VB)
        pltpu.make_async_copy(s_scr.at[k], g.at[pos("y"), :, here], local).start()
        wait(s_scr.at[k], local)


    def areas(k, color, phase, v, half=None):
        order, rows = COLORS[color]
        place = {a: pos(a) for a in "xyz"}
        for a in order[:phase]:
            place[a] = None
        place[order[phase]] = v
        row0, n = sum(sum(c[1]) for c in COLORS[:color]), sum(rows)
        if half is not None:
            row0, n = row0 + half * rows[0], rows[half]
        ys = slice(None) if place["y"] is None else pl.ds(place["y"], 1)
        for z in range(N["z"]) if place["z"] is None else (place["z"],):
            col, width = z * quarter + k * wg, wg
            if place["x"] is not None:
                col, width = col + place["x"] * VB, VB
            yield g.at[ys, pl.ds(row0, n), pl.ds(pl.multiple_of(col, LANES), width)]

    def units(color, phase):
        n = 1
        for a in COLORS[color][0][:phase]:
            n *= N[a]
        return n

    def bulk(color, count, part=None):
        rows = COLORS[color][1]
        n = sum(rows) if part is None else rows[part]
        return g.at[0, pl.ds(0, n), pl.ds(0, count * VB)]

    def near(k, c, phase):
        axis = COLORS[c][0][phase]
        if phase > 0:
            far_done(k, c, phase - 1)
        if N[axis] > 1:
            for _, by in BOTH:
                for src in areas(k, c, phase, pos(axis)):
                    push(src, src, ag_send.at[k, c], ag_recv.at[k, c, 2 * phase], axis, by)

    def far(k, c, phase):
        axis = COLORS[c][0][phase]
        if N[axis] > 1:
            wait(bulk(c, 2 * units(c, phase)), ag_recv.at[k, c, 2 * phase])
            for half, by in BOTH:
                for src in areas(k, c, phase, pos(axis, N[axis] - by), half):
                    push(src, src, ag_send.at[k, c], ag_recv.at[k, c, 2 * phase + 1], axis, by)

    def far_done(k, c, phase):
        if N[COLORS[c][0][phase]] > 1:
            wait(bulk(c, units(c, phase)), ag_recv.at[k, c, 2 * phase + 1])

    def gather_end(k, c):
        far_done(k, c, 2)
        count = sum(3 * units(c, i) for i in TRIPLE if N[COLORS[c][0][i]] > 1)
        wait(bulk(c, count), ag_send.at[k, c])

    reduces = (reduce_start, reduce_pass, reduce_turn, reduce_pass2, reduce_end)

    def stage(index, tick, *args):
        since = slot - 1 - index

        @pl.when((since >= 0) & (lax.rem(since, 2) == 0) & (since < 2 * K))
        def _():
            tick(since // 2, *args)

    def fetch(i):
        pltpu.make_async_copy(z_hbm.at[:, pl.ds(pl.multiple_of(i * DVB, LANES), DVB)], zb, z_sem).start()

    @pl.when(slot == 0)
    def _():
        fetch(0)
        for r in range(N["z"]):
            for k in TRIPLE:
                st[k, r * T : (r + 1) * T, :] = spread(rows_ref[r, k : k + 1, :])
        acc[...] = jnp.zeros_like(acc)
        found[...] = jnp.zeros_like(found)
        enter()

    for i, tick in enumerate(reduces):
        stage(i, tick)
    for c in range(len(COLORS)):
        for phase in TRIPLE:
            stage(len(reduces) + 2 * phase, near, c, phase)
            stage(len(reduces) + 2 * phase + 1, far, c, phase)
        stage(len(reduces) + 6, gather_end, c)

    hit_value = rows_ref[0, 4:5, :LANES]

    @pl.when((slot < 2 * K) & (lax.rem(slot, 2) == 0))
    def _():
        k = slot // 2
        buf = lax.rem(k, NP)
        base = lax.axis_index("tp") * VSH + lax.axis_index("z") * quarter + k * wg
        ids = (lax.broadcasted_iota(jnp.int32, (16, wg), 1) + base).astype(F32)
        hit_row = jnp.concatenate([hit_value] * nx, axis=1)

        def logits(h, t0):
            zs[h] = dot(u_ref[pl.ds(t0, HALF), :], eg_ref[...])

        def deltas(h, t0):
            for r in range(0, HALF, 16):
                here = pl.ds(t0 + r, 16)
                top, scale, label = (jnp.concatenate([st[i, here, :]] * nx, axis=1) for i in TRIPLE)
                e = jnp.exp(zs[h, r : r + 16, :] - top) * scale
                ds[h, r : r + 16, :] = jnp.where(label == ids, e - hit_row, e).astype(BF16)

        def product(h, t0):
            part = dot(ut_ref[:, pl.ds(t0, HALF)], ds[h]).reshape(ny, YR, wg)
            for i in range(nx):
                p[buf, i] += part[:, :, i * VB : (i + 1) * VB]

        p[buf] = jnp.zeros(p.shape[1:], F32)

        @pl.loop(0, N["z"])
        def _(r):
            ta = pl.multiple_of(r * T, T)
            tb = pl.multiple_of(r * T + HALF, HALF)
            logits(0, ta)
            logits(1, tb)
            deltas(0, ta)
            product(0, ta)
            deltas(1, tb)
            product(1, tb)

    @pl.when((slot < 2 * dus) & (lax.rem(slot, 2) == 1))
    def _():
        i = slot // 2
        wait(zb, z_sem)
        base = lax.axis_index("tp") * VSH + i * DVB
        ids0 = lax.broadcasted_iota(jnp.int32, (32, LANES), 1) + base
        for k in range(DVB // SUB):
            cols = slice(k * SUB, (k + 1) * SUB)
            ids = [(ids0 + j).astype(F32) for j in range(k * SUB, (k + 1) * SUB, LANES)]
            for r in range(0, T, 32):
                here = slice(r, r + 32)
                top, scale, label = (st[n, here, :] for n in TRIPLE)
                hits = found[here, :]
                for j, idj in enumerate(ids):
                    z = zb[here, k * SUB + j * LANES : k * SUB + (j + 1) * LANES]
                    e = jnp.exp(z - top) * scale
                    hit = label == idj
                    hits = hits + jnp.where(hit, z, 0.0)
                    dd[k % 2, here, j * LANES : (j + 1) * LANES] = jnp.where(hit, e - hit_value, e).astype(BF16)
                found[here, :] = hits
            acc[:, :D] += dot_nt(dd[k % 2], ed_ref[:, cols])

        @pl.when(i + 1 < dus)
        def _():
            fetch(i + 1)


    def finish_du():
        if N["tp"] > 1:
            push(acc, du.at[1], d_send.at[0], d_recv, "tp", 1)
        pltpu.make_async_copy(acc, du.at[0], d_send.at[1]).start()
        logs = jnp.where(lax.axis_index("tp") == 0, jnp.sum(rows_ref[0, 3:4, :]), 0.0)
        own[0] = jnp.broadcast_to(logs - jnp.sum(found[...]), own.shape[1:])

    def finish():
        wait(acc, d_send.at[1])
        if N["tp"] > 1:
            wait(acc, d_send.at[0])
            wait(acc, d_recv)
        loss_ref[...] = own[len(AXES)] * hit_value

    pl.when(slot == 2 * dus)(finish_du)
    for i in range(len(AXES) + 1):
        pl.when(slot == 2 * dus + 1 + i)(functools.partial(total, i, AXES, own, got, l_send, l_recv))
    pl.when(slot == pl.num_programs(0) - 1)(finish)


AXES = ("tp", "x", "y", "z")


def main_call(rows, u_all, ut_all, emb_t, logits):
    nx, ny, nz = N["x"], N["y"], N["z"]
    wg = nx * VB
    dus = VSH // DVB
    dma = pltpu.SemaphoreType.DMA

    def grad_block(s):
        return 0, lax.axis_index("z") * K + jnp.minimum(s // 2, K - 1)

    def du_block(s):
        return 0, jnp.minimum(s // 2, dus - 1)

    once = dict(pipeline_mode=pl.Buffered(1))
    return pl.pallas_call(
        main_kernel,
        grid=(2 * K + 12,),
        in_specs=[
            whole((nz, 8, T), **once),
            whole((nz * T, D), **once),
            whole((D, nz * T), **once),
            pl.BlockSpec((D, wg), grad_block),
            pl.BlockSpec((D, DVB), du_block),
            ANY,
        ],
        out_specs=[ANY, ANY, whole((8, LANES))],
        out_shape=[
            jax.ShapeDtypeStruct((ny, YR, VSH), F32),
            jax.ShapeDtypeStruct((2, T, DP), F32),
            jax.ShapeDtypeStruct((8, LANES), F32),
        ],
        scratch_shapes=[
            pltpu.VMEM(shape, F32)
            for shape in (
                (3, nz * T, LANES),
                (2, HALF, wg),
            )
        ]
        + [pltpu.VMEM((2, HALF, wg), BF16)]
        + [
            pltpu.VMEM(shape, F32)
            for shape in (
                (NP, nx, ny, YR, VB),
                (K, 2, 2, 2, RH, VB),
                (K, 2, 2, 4, RH, VB),
                (K, 2, RH, VB),
                (K, 2, 2, RH, VB),
                (NP, 2, 4, RH, VB),
                (K, YR, VB),
                (T, DVB),
                (T, DP),
            )
        ]
        + [
            pltpu.VMEM((2, T, SUB), BF16),
            pltpu.VMEM((T, LANES), F32),
            pltpu.VMEM((5, 8, LANES), F32),
            pltpu.VMEM((4, 3, 8, LANES), F32),
            dma((K, 2)),
            dma((K, 2, 4)),
            dma((K, 3)),
            dma((K, 3, 6)),
            dma((4, 3)),
            dma((4, 3)),
            dma((2,)),
            dma,
            dma,
            dma,
        ],
        compiler_params=params(collective_id=2, has_side_effects=True),
        cost_estimate=cost(6 * T * D * VSH, T * VSH * 4),
        name="main",
    )(rows, u_all, ut_all, emb_t, emb_t, logits)


def solution(mesh):
    axes = tuple(N)
    grid_mesh = Mesh(mesh.devices.reshape(tuple(N.values())), axes)

    def local_body(hidden, labels, loss_mask, norm_gain, embedding):
        emb_t = embedding.T
        hid_t = hidden.transpose(0, 2, 1)
        gain = norm_gain.astype(F32)[:, None]
        u, ut, pay = norm_call(hid_t, gain)
        logits, rows, ug = stats_call(pay, loss_mask, labels, u, emb_t)
        u_all, ut_all = pack_call(u, ut, ug)
        grad, du, loss = main_call(rows, u_all, ut_all, emb_t, logits)
        d_hidden = norm_back_call(hid_t, gain, du)
        return loss[0, 0], d_hidden.transpose(0, 2, 1), grad.reshape(D, VSH).T

    dp = axes[1:]
    return jax.shard_map(
        local_body,
        mesh=grid_mesh,
        in_specs=(P(dp), P(dp), P(dp), P(), P("tp")),
        out_specs=(P(), P(dp), P("tp")),
        check_vma=False,
    )
```

time: 951 us -> 481 us (0.51)
  waiting for transfers between devices: 472 us -> 0 us
  Pallas kernels: 0 us -> 439 us
  blocking collectives: 186 us -> 0 us
  matrix products: 135 us -> 0 us
  other arithmetic: 95.2 us -> 0 us
  between operations: 16.7 us -> 0.65 us
    psum x2 -> x0, waiting for transfers between devices: 472 us -> none  [the longest x1 472 us: local_body(): grad_embed = lax.psum(grad_part, 'dpcp')]
    pallas_call x0 -> x5, Pallas kernels: none -> 439 us  [the longest x1 341 us: main_call(): pl.pallas_call(main_kernel, grid=(2 * K + 12,), in_specs=[whole((nz, 8, T...]
    psum x2 -> x0, blocking collectives: 184 us -> none  [the longest x1 181 us: local_body(): total_loss = lax.psum(jnp.sum(tok_mask * tok_loss), 'dpcp') / mask_count]
    dot_general x3 -> x0, matrix products: 135 us -> none  [the longest x1 52.3 us: local_body(): lax.dot_general(normed, embedding, (((1,), (1,)), ((), ())), preferred_el...]
    convert_element_type x3 -> x0, other arithmetic: 49.8 us -> none  [the longest x1 49.3 us: local_body(): (jnp.where(is_label, prob_vals - 1.0, prob_vals) * (tok_mask / mask_count...]
    reduce_sum x5 -> x0, other arithmetic: 41.5 us -> none  [the longest x1 36.6 us: local_body(): jnp.sum(exp_vals, axis=-1)]
    unnamed x28 -> x1, local copies, waits for them, and re-layouts: 42.1 us -> 38.5 us
  transfers between devices with their start and end apart: 2 -> 0, of which waited for: 1 -> 0; matrix products, arithmetic and copies ran while one was open for 5% -> 0% of each run, Pallas kernels for 0% -> 0%
where the time goes in v2:
time: 481 us
  Pallas kernels  439 us (91%)
  local copies, waits for them, and re-layouts  41.2 us (9%)
    pallas_call x1, Pallas kernels, main_call(): pl.pallas_call(main_kernel, grid=(2 * K + 12,), in_specs=[whole((nz, 8, T...  341 us
    pallas_call x1, Pallas kernels, stats_call(): pl.pallas_call(stats_kernel, grid=(VSH // SVB,), in_specs=[ANY, whole((2,...  80.7 us
    unnamed x1, local copies, waits for them, and re-layouts  38.5 us

profile of v2, /device:TPU:0, one launch (start us, length us, event | category | flops | bytes accessed | tf_op | source)
XLA Modules:
  0.0 480.7 jit_solution(4957351841673044003)
XLA Ops:
  0.6 1.5 reshape.11.g_ref
  2.2 3.5 norm.1
  5.6 80.7 %stats.1 = (f32[1024,24576]{1,0:T(8,128)}, f32[4,8,1024]{2,1,0:T(8,128)}, f32[2,3,576,512]{3,2,1,0:T(8,128)}) custom-call(f32[576,512]{1,0:T(8,128)} %get-tuple-element.14.pay, s32[2,512]{1,0:T(2,128)} %mask_ref.1, s32[2,512]{1,0:T(2,128)} %lab_ref.1, bf16[1024,576]{1,0:T(8,128)(2,1)} %get-tuple-element.15.u_ref, bf16[576,24576]{1,0:T(8,128)(2,1)} %bitcast.11), custom_call_target="tpu_custom_call" | custom-call | flops 28991029248 | bytes 100663296 | tf_op jit(solution)/shard_map/stats/pallas_call | solution.py:279
  86.3 8.7 %pack.1 = (bf16[4096,576]{1,0:T(8,128)(2,1)}, bf16[576,4096]{1,0:T(8,128)(2,1)}) custom-call(bf16[1024,576]{1,0:T(8,128)(2,1)} %get-tuple-element.15.u_ref, bf16[576,1024]{1,0:T(8,128)(2,1)} %get-tuple-element.17.ut_ref, f32[2,3,576,512]{3,2,1,0:T(8,128)} %get-tuple-element.18.own_ref.sib_ref, f32[2,3,576,512]{3,2,1,0:T(8,128)} %get-tuple-element.18.own_ref.sib_ref), custom_call_target="tpu_custom_call" | custom-call | tf_op jit(solution)/shard_map/pack/pallas_call | solution.py:335
  95.1 341.3 %main.1 = (f32[4,144,24576]{2,1,0:T(8,128)}, f32[2,1024,640]{2,1,0:T(8,128)}, f32[8,128]{1,0:T(8,128)}) custom-call(f32[4,8,1024]{2,1,0:T(8,128)} %get-tuple-element.16.rows_ref, bf16[4096,576]{1,0:T(8,128)(2,1)} %get-tuple-element.19.u_ref, bf16[576,4096]{1,0:T(8,128)(2,1)} %get-tuple-element.20.ut_ref, bf16[576,24576]{1,0:T(8,128)(2,1)} %bitcast.12, ...), custom_call_target="tpu_custom_call" | custom-call | flops 86973087744 | bytes 100663296 | tf_op jit(solution)/shard_map/main/pallas_call | solution.py:608
  436.4 1.2 slice.3
  437.6 4.7 norm_back.1
  442.3 38.5 %copy.11 = f32[24576,576]{0,1:T(8,128)} copy(f32[24576,576]{0,1:T(8,128)} %bitcast.7) | data formatting | bytes 113246208

commit v3 on v2

--- a/solution.py
+++ b/solution.py
@@ -22,12 +22,14 @@
 YR = 144
 RH = 72
 LANES = 128
-NEG = -3.0e38
-COLORS = (("yzx", (24, 24)), ("xzy", (24, 24)), ("xyz", (24, 24)))
+HUGE = 3.0e38
+LOG2E, LN2 = 1.4426950408889634, 0.6931471805599453
+COLORS = (("yzx", (24, 24)), ("xzy", (24, 24)), ("xyz", (16, 8)), ("yxz", (8, 16)))
 BOTH = ((0, 1), (1, 3))
 F32, BF16 = jnp.float32, jnp.bfloat16
 FAR = (1, 3, 2)
 PAIR, TRIPLE = range(2), range(3)
+FEW, SOME = 16, 32
 
 
 def mean0(x):
@@ -169,9 +171,9 @@
 
 
 def stats_kernel(
-    pay, mask_ref, lab_ref, u_ref, e_ref, z_ref, rows_ref, ug, m_scr, s_scr, own, got, ms, rows_got, *sems
+    pay, mask_ref, lab_ref, u_ref, e_ref, z_ref, rows_ref, out, m_scr, s_scr, own, got, ms, rows_got, ug, *sems
 ):
-    c_send, c_recv, u_send, u_recv, r_send, r_recv = sems
+    c_send, c_recv, u_send, u_recv, r_send, r_recv, local = sems
     step, steps = pl.program_id(0), pl.num_programs(0)
     cut = D // 2
     near = ((1, 0), (3, 1))
@@ -179,8 +181,11 @@
     def at(index, tick):
         pl.when(step == index)(tick)
 
+    def keep(*place):
+        pltpu.make_async_copy(ug.at[place], out.at[place], local.at[place]).start()
+
     def begin():
-        m_scr[...] = jnp.full_like(m_scr, NEG)
+        m_scr[...] = jnp.full_like(m_scr, -HUGE)
         s_scr[...] = jnp.zeros_like(s_scr)
         own[0] = jnp.broadcast_to(jnp.sum(mask_ref[...].astype(F32)), own.shape[1:])
         enter()
@@ -196,6 +201,7 @@
             for by, i in near:
                 piece = pl.ds(i * cut, cut)
                 push(ug.at[0, i, piece], ug.at[0, 2, piece], u_send.at[0, 2 + i], u_recv.at[0, 2 + i], "z", by)
+                keep(0, i)
                 if N["tp"] > 1:
                     push(ug.at[0, i], ug.at[1, i], u_send.at[1, i], u_recv.at[1, i], "tp", 1)
 
@@ -203,8 +209,12 @@
         if N["z"] > 1:
             for i in PAIR:
                 wait(ug.at[0, 2, pl.ds(i * cut, cut)], u_recv.at[0, 2 + i])
+            keep(0, 2)
             if N["tp"] > 1:
                 push(ug.at[0, 2], ug.at[1, 2], u_send.at[1, 2], u_recv.at[1, 2], "tp", 1)
+                for i in PAIR:
+                    wait(ug.at[1, i], u_recv.at[1, i])
+                    keep(1, i)
 
     at(0, begin)
     for i in range(1, 4):
@@ -213,19 +223,19 @@
     at(steps - 1, share_far)
 
     def fold(k):
-        for r in range(0, T, 64):
-            rows = slice(r, r + 64)
+        for r in range(0, T, SOME):
+            rows = slice(r, r + SOME)
             parts = [z_ref[rows, j : j + LANES] for j in range(k * SUB, (k + 1) * SUB, LANES)]
             old = m_scr[rows, :]
             new = functools.reduce(jnp.maximum, parts, old)
-            acc = s_scr[rows, :] * jnp.exp(old - new)
+            acc = s_scr[rows, :] * jnp.exp2(old - new)
             for p in parts:
-                acc = acc + jnp.exp(p - new)
+                acc = acc + jnp.exp2(p - new)
             m_scr[rows, :] = new
             s_scr[rows, :] = acc
 
     for k in range(SVB // SUB):
-        z_ref[:, k * SUB : (k + 1) * SUB] = dot(u_ref[...], e_ref[:, k * SUB : (k + 1) * SUB])
+        z_ref[:, k * SUB : (k + 1) * SUB] = dot(u_ref[...], e_ref[:, k * SUB : (k + 1) * SUB]) * LOG2E
         if k:
             fold(k - 1)
     fold(SVB // SUB - 1)
@@ -234,7 +244,7 @@
     def _():
         m_lane = m_scr[...]
         m_row = fold1(jnp.max, m_lane)
-        s_row = fold1(jnp.sum, s_scr[...] * jnp.exp(m_lane - m_row))
+        s_row = fold1(jnp.sum, s_scr[...] * jnp.exp2(m_lane - m_row))
         for i, row in enumerate((m_row, s_row)):
             ms[0, 8 * i : 8 * (i + 1)] = jnp.broadcast_to(row, (T, LANES)).T[:8]
         if N["tp"] > 1:
@@ -242,7 +252,7 @@
             wait(ms.at[1], r_recv.at[3])
             wait(ms.at[0], r_send.at[3])
         count = own[3, :1, :1]
-        rows_ref[0, 4:8, :] = jnp.broadcast_to(1.0 / count, (4, T))
+        rows_ref[0, 3:8, :] = jnp.broadcast_to(1.0 / count, (5, T))
         swap = lax.axis_index("tp") == 1
         for k in PAIR:
             here = slice(k * HALF, (k + 1) * HALF)
@@ -251,12 +261,13 @@
             if N["tp"] > 1:
                 m1, m2 = top, ms[1, :1, here]
                 top = jnp.maximum(m1, m2)
-                a, b = whole_sum * jnp.exp(m1 - top), ms[1, 8:9, here] * jnp.exp(m2 - top)
+                a, b = whole_sum * jnp.exp2(m1 - top), ms[1, 8:9, here] * jnp.exp2(m2 - top)
                 whole_sum = jnp.where(swap, b + a, a + b)
-            rows_ref[0, :1, here] = top
-            rows_ref[0, 1:2, here] = mask / count / whole_sum
-            rows_ref[0, 2:3, here] = jnp.where(mask > 0.0, lab_ref[k : k + 1, :].astype(F32), -1.0)
-            rows_ref[0, 3:4, here] = mask * (top + jnp.log(whole_sum))
+            counts = mask > 0.0
+            lse = top + jnp.log(whole_sum) * LOG2E
+            rows_ref[0, :1, here] = jnp.where(counts, lse + jnp.log(count) * LOG2E, HUGE)
+            rows_ref[0, 1:2, here] = jnp.where(counts, lab_ref[k : k + 1, :].astype(F32), -1.0)
+            rows_ref[0, 2:3, here] = mask * lse * LN2
         rows_got[0] = rows_ref[0]
         for i, by in enumerate(peers("z")):
             push(rows_got.at[0], rows_got.at[1 + i], r_send.at[i], r_recv.at[i], "z", by)
@@ -269,9 +280,13 @@
                 wait(pay, u_send.at[0, i])
                 wait(ug.at[0, 2, pl.ds(i * cut, cut)], u_send.at[0, 2 + i])
             if N["tp"] > 1:
+                wait(ug.at[1, 2], u_recv.at[1, 2])
+                keep(1, 2)
                 for i in TRIPLE:
                     wait(ug.at[0, i], u_send.at[1, i])
-                    wait(ug.at[1, i], u_recv.at[1, i])
+                    wait(ug.at[1, i], local.at[1, i])
+            for i in TRIPLE:
+                wait(ug.at[0, i], local.at[0, i])
 
 
 def stats_call(pay, mask, lab, u, emb_t):
@@ -280,7 +295,7 @@
         stats_kernel,
         grid=(VSH // SVB,),
         in_specs=[
-            ANY,
+            whole((D, HALF)),
             whole((2, HALF)),
             whole((2, HALF)),
             whole((T, D)),
@@ -299,12 +314,14 @@
             pltpu.VMEM((3, 3, 8, LANES), F32),
             pltpu.VMEM((2, 16, T), F32),
             pltpu.VMEM((4, 8, T), F32),
+            pltpu.VMEM((2, 3, D, HALF), F32),
             dma((3, 3)),
             dma((3, 3)),
             dma((2, 4)),
             dma((2, 4)),
             dma((4,)),
             dma((4,)),
+            dma((2, 3)),
         ],
         compiler_params=params(collective_id=1, has_side_effects=True),
         cost_estimate=cost(2 * T * D * VSH, T * VSH * 4),
@@ -490,39 +507,39 @@
     def _():
         fetch(0)
         for r in range(N["z"]):
-            for k in TRIPLE:
+            for k in PAIR:
                 st[k, r * T : (r + 1) * T, :] = spread(rows_ref[r, k : k + 1, :])
         acc[...] = jnp.zeros_like(acc)
         found[...] = jnp.zeros_like(found)
         enter()
 
-    for i, tick in enumerate(reduces):
-        stage(i, tick)
     for c in range(len(COLORS)):
         for phase in TRIPLE:
             stage(len(reduces) + 2 * phase, near, c, phase)
             stage(len(reduces) + 2 * phase + 1, far, c, phase)
         stage(len(reduces) + 6, gather_end, c)
-
-    hit_value = rows_ref[0, 4:5, :LANES]
+    for i, tick in enumerate(reduces):
+        stage(i, tick)
+
+    hit_value = rows_ref[0, 3:4, :LANES]
 
     @pl.when((slot < 2 * K) & (lax.rem(slot, 2) == 0))
     def _():
         k = slot // 2
         buf = lax.rem(k, NP)
         base = lax.axis_index("tp") * VSH + lax.axis_index("z") * quarter + k * wg
-        ids = (lax.broadcasted_iota(jnp.int32, (16, wg), 1) + base).astype(F32)
+        ids = (lax.broadcasted_iota(jnp.int32, (FEW, wg), 1) + base).astype(F32)
         hit_row = jnp.concatenate([hit_value] * nx, axis=1)
 
         def logits(h, t0):
             zs[h] = dot(u_ref[pl.ds(t0, HALF), :], eg_ref[...])
 
         def deltas(h, t0):
-            for r in range(0, HALF, 16):
-                here = pl.ds(t0 + r, 16)
-                top, scale, label = (jnp.concatenate([st[i, here, :]] * nx, axis=1) for i in TRIPLE)
-                e = jnp.exp(zs[h, r : r + 16, :] - top) * scale
-                ds[h, r : r + 16, :] = jnp.where(label == ids, e - hit_row, e).astype(BF16)
+            for r in range(0, HALF, FEW):
+                here = pl.ds(t0 + r, FEW)
+                lse, label = (jnp.concatenate([st[i, here, :]] * nx, axis=1) for i in PAIR)
+                e = jnp.exp2(zs[h, r : r + FEW, :] * LOG2E - lse)
+                ds[h, r : r + FEW, :] = jnp.where(label == ids, e - hit_row, e).astype(BF16)
 
         def product(h, t0):
             part = dot(ut_ref[:, pl.ds(t0, HALF)], ds[h]).reshape(ny, YR, wg)
@@ -547,19 +564,19 @@
         i = slot // 2
         wait(zb, z_sem)
         base = lax.axis_index("tp") * VSH + i * DVB
-        ids0 = lax.broadcasted_iota(jnp.int32, (32, LANES), 1) + base
+        ids0 = lax.broadcasted_iota(jnp.int32, (SOME, LANES), 1) + base
         for k in range(DVB // SUB):
             cols = slice(k * SUB, (k + 1) * SUB)
             ids = [(ids0 + j).astype(F32) for j in range(k * SUB, (k + 1) * SUB, LANES)]
-            for r in range(0, T, 32):
-                here = slice(r, r + 32)
-                top, scale, label = (st[n, here, :] for n in TRIPLE)
+            for r in range(0, T, SOME):
+                here = slice(r, r + SOME)
+                lse, label = (st[n, here, :] for n in PAIR)
                 hits = found[here, :]
                 for j, idj in enumerate(ids):
                     z = zb[here, k * SUB + j * LANES : k * SUB + (j + 1) * LANES]
-                    e = jnp.exp(z - top) * scale
+                    e = jnp.exp2(z - lse)
                     hit = label == idj
-                    hits = hits + jnp.where(hit, z, 0.0)
+                    hits = jnp.where(hit, z, hits)
                     dd[k % 2, here, j * LANES : (j + 1) * LANES] = jnp.where(hit, e - hit_value, e).astype(BF16)
                 found[here, :] = hits
             acc[:, :D] += dot_nt(dd[k % 2], ed_ref[:, cols])
@@ -573,8 +590,8 @@
         if N["tp"] > 1:
             push(acc, du.at[1], d_send.at[0], d_recv, "tp", 1)
         pltpu.make_async_copy(acc, du.at[0], d_send.at[1]).start()
-        logs = jnp.where(lax.axis_index("tp") == 0, jnp.sum(rows_ref[0, 3:4, :]), 0.0)
-        own[0] = jnp.broadcast_to(logs - jnp.sum(found[...]), own.shape[1:])
+        logs = jnp.where(lax.axis_index("tp") == 0, jnp.sum(rows_ref[0, 2:3, :]), 0.0)
+        own[0] = jnp.broadcast_to(logs - jnp.sum(found[...]) * LN2, own.shape[1:])
 
     def finish():
         wait(acc, d_send.at[1])
@@ -625,7 +642,7 @@
         scratch_shapes=[
             pltpu.VMEM(shape, F32)
             for shape in (
-                (3, nz * T, LANES),
+                (2, nz * T, LANES),
                 (2, HALF, wg),
             )
         ]
@@ -651,8 +668,8 @@
             pltpu.VMEM((4, 3, 8, LANES), F32),
             dma((K, 2)),
             dma((K, 2, 4)),
-            dma((K, 3)),
-            dma((K, 3, 6)),
+            dma((K, len(COLORS))),
+            dma((K, len(COLORS), 6)),
             dma((4, 3)),
             dma((4, 3)),
             dma((2,)),

time: 481 us -> 471 us (0.979)
  Pallas kernels: 439 us -> 429 us
    pallas_call x1, Pallas kernels: 341 us -> 328 us  [main_call(): pl.pallas_call(main_kernel, grid=(2 * K + 12,), in_specs=[whole((nz, 8, T...]
where the time goes in v3:
time: 471 us
  Pallas kernels  429 us (91%)
  local copies, waits for them, and re-layouts  41.2 us (9%)
    pallas_call x1, Pallas kernels, main_call(): pl.pallas_call(main_kernel, grid=(2 * K + 12,), in_specs=[whole((nz, 8, T...  328 us
    pallas_call x1, Pallas kernels, stats_call(): pl.pallas_call(stats_kernel, grid=(VSH // SVB,), in_specs=[whole((D, HALF...  84.3 us
    unnamed x1, local copies, waits for them, and re-layouts  38.5 us

profile of v3, /device:TPU:0, one launch (start us, length us, event | category | flops | bytes accessed | tf_op | source)
XLA Modules:
  0.0 470.6 jit_solution(2106165013947006002)
XLA Ops:
  0.6 1.5 reshape.11.g_ref
  2.2 3.5 norm.1
  5.6 84.3 %stats.1 = (f32[1024,24576]{1,0:T(8,128)}, f32[4,8,1024]{2,1,0:T(8,128)}, f32[2,3,576,512]{3,2,1,0:T(8,128)}) custom-call(f32[576,512]{1,0:T(8,128)} %get-tuple-element.14.pay, s32[2,512]{1,0:T(2,128)} %mask_ref.1, s32[2,512]{1,0:T(2,128)} %lab_ref.1, bf16[1024,576]{1,0:T(8,128)(2,1)} %get-tuple-element.15.u_ref, bf16[576,24576]{1,0:T(8,128)(2,1)} %bitcast.11), custom_call_target="tpu_custom_call" | custom-call | flops 28991029248 | bytes 100663296 | tf_op jit(solution)/shard_map/stats/pallas_call | solution.py:294
  90.0 8.7 %pack.1 = (bf16[4096,576]{1,0:T(8,128)(2,1)}, bf16[576,4096]{1,0:T(8,128)(2,1)}) custom-call(bf16[1024,576]{1,0:T(8,128)(2,1)} %get-tuple-element.15.u_ref, bf16[576,1024]{1,0:T(8,128)(2,1)} %get-tuple-element.17.ut_ref, f32[2,3,576,512]{3,2,1,0:T(8,128)} %get-tuple-element.18.own_ref.sib_ref, f32[2,3,576,512]{3,2,1,0:T(8,128)} %get-tuple-element.18.own_ref.sib_ref), custom_call_target="tpu_custom_call" | custom-call | tf_op jit(solution)/shard_map/pack/pallas_call | solution.py:352
  98.7 327.6 %main.1 = (f32[4,144,24576]{2,1,0:T(8,128)}, f32[2,1024,640]{2,1,0:T(8,128)}, f32[8,128]{1,0:T(8,128)}) custom-call(f32[4,8,1024]{2,1,0:T(8,128)} %get-tuple-element.16.rows_ref, bf16[4096,576]{1,0:T(8,128)(2,1)} %get-tuple-element.19.u_ref, bf16[576,4096]{1,0:T(8,128)(2,1)} %get-tuple-element.20.ut_ref, bf16[576,24576]{1,0:T(8,128)(2,1)} %bitcast.12, ...), custom_call_target="tpu_custom_call" | custom-call | flops 86973087744 | bytes 100663296 | tf_op jit(solution)/shard_map/main/pallas_call | solution.py:625
  426.3 1.2 slice.3
  427.5 4.7 norm_back.1
  432.1 38.5 %copy.11 = f32[24576,576]{0,1:T(8,128)} copy(f32[24576,576]{0,1:T(8,128)} %bitcast.7) | data formatting | bytes 113246208

commit v4 on v3

--- a/solution.py
+++ b/solution.py
@@ -23,7 +23,6 @@
 RH = 72
 LANES = 128
 HUGE = 3.0e38
-LOG2E, LN2 = 1.4426950408889634, 0.6931471805599453
 COLORS = (("yzx", (24, 24)), ("xzy", (24, 24)), ("xyz", (16, 8)), ("yxz", (8, 16)))
 BOTH = ((0, 1), (1, 3))
 F32, BF16 = jnp.float32, jnp.bfloat16
@@ -217,8 +216,8 @@
                     keep(1, i)
 
     at(0, begin)
-    for i in range(1, 4):
-        at(i, functools.partial(total, i, "xyz", own, got, c_send, c_recv))
+    for i, when in enumerate((1, 2, steps - 2)):
+        at(when, functools.partial(total, i + 1, "xyz", own, got, c_send, c_recv))
     at(steps * 7 // 12, pass_on)
     at(steps - 1, share_far)
 
@@ -228,14 +227,14 @@
             parts = [z_ref[rows, j : j + LANES] for j in range(k * SUB, (k + 1) * SUB, LANES)]
             old = m_scr[rows, :]
             new = functools.reduce(jnp.maximum, parts, old)
-            acc = s_scr[rows, :] * jnp.exp2(old - new)
+            acc = s_scr[rows, :] * jnp.exp(old - new)
             for p in parts:
-                acc = acc + jnp.exp2(p - new)
+                acc = acc + jnp.exp(p - new)
             m_scr[rows, :] = new
             s_scr[rows, :] = acc
 
     for k in range(SVB // SUB):
-        z_ref[:, k * SUB : (k + 1) * SUB] = dot(u_ref[...], e_ref[:, k * SUB : (k + 1) * SUB]) * LOG2E
+        z_ref[:, k * SUB : (k + 1) * SUB] = dot(u_ref[...], e_ref[:, k * SUB : (k + 1) * SUB])
         if k:
             fold(k - 1)
     fold(SVB // SUB - 1)
@@ -244,7 +243,7 @@
     def _():
         m_lane = m_scr[...]
         m_row = fold1(jnp.max, m_lane)
-        s_row = fold1(jnp.sum, s_scr[...] * jnp.exp2(m_lane - m_row))
+        s_row = fold1(jnp.sum, s_scr[...] * jnp.exp(m_lane - m_row))
         for i, row in enumerate((m_row, s_row)):
             ms[0, 8 * i : 8 * (i + 1)] = jnp.broadcast_to(row, (T, LANES)).T[:8]
         if N["tp"] > 1:
@@ -261,13 +260,13 @@
             if N["tp"] > 1:
                 m1, m2 = top, ms[1, :1, here]
                 top = jnp.maximum(m1, m2)
-                a, b = whole_sum * jnp.exp2(m1 - top), ms[1, 8:9, here] * jnp.exp2(m2 - top)
+                a, b = whole_sum * jnp.exp(m1 - top), ms[1, 8:9, here] * jnp.exp(m2 - top)
                 whole_sum = jnp.where(swap, b + a, a + b)
             counts = mask > 0.0
-            lse = top + jnp.log(whole_sum) * LOG2E
-            rows_ref[0, :1, here] = jnp.where(counts, lse + jnp.log(count) * LOG2E, HUGE)
+            lse = top + jnp.log(whole_sum)
+            rows_ref[0, :1, here] = jnp.where(counts, lse + jnp.log(count), HUGE)
             rows_ref[0, 1:2, here] = jnp.where(counts, lab_ref[k : k + 1, :].astype(F32), -1.0)
-            rows_ref[0, 2:3, here] = mask * lse * LN2
+            rows_ref[0, 2:3, here] = mask * lse
         rows_got[0] = rows_ref[0]
         for i, by in enumerate(peers("z")):
             push(rows_got.at[0], rows_got.at[1 + i], r_send.at[i], r_recv.at[i], "z", by)
@@ -538,7 +537,7 @@
             for r in range(0, HALF, FEW):
                 here = pl.ds(t0 + r, FEW)
                 lse, label = (jnp.concatenate([st[i, here, :]] * nx, axis=1) for i in PAIR)
-                e = jnp.exp2(zs[h, r : r + FEW, :] * LOG2E - lse)
+                e = jnp.exp(zs[h, r : r + FEW, :] - lse)
                 ds[h, r : r + FEW, :] = jnp.where(label == ids, e - hit_row, e).astype(BF16)
 
         def product(h, t0):
@@ -574,7 +573,7 @@
                 hits = found[here, :]
                 for j, idj in enumerate(ids):
                     z = zb[here, k * SUB + j * LANES : k * SUB + (j + 1) * LANES]
-                    e = jnp.exp2(z - lse)
+                    e = jnp.exp(z - lse)
                     hit = label == idj
                     hits = jnp.where(hit, z, hits)
                     dd[k % 2, here, j * LANES : (j + 1) * LANES] = jnp.where(hit, e - hit_value, e).astype(BF16)
@@ -591,7 +590,7 @@
             push(acc, du.at[1], d_send.at[0], d_recv, "tp", 1)
         pltpu.make_async_copy(acc, du.at[0], d_send.at[1]).start()
         logs = jnp.where(lax.axis_index("tp") == 0, jnp.sum(rows_ref[0, 2:3, :]), 0.0)
-        own[0] = jnp.broadcast_to(logs - jnp.sum(found[...]) * LN2, own.shape[1:])
+        own[0] = jnp.broadcast_to(logs - jnp.sum(found[...]), own.shape[1:])
 
     def finish():
         wait(acc, d_send.at[1])
@@ -602,7 +601,7 @@
 
     pl.when(slot == 2 * dus)(finish_du)
     for i in range(len(AXES) + 1):
-        pl.when(slot == 2 * dus + 1 + i)(functools.partial(total, i, AXES, own, got, l_send, l_recv))
+        pl.when(slot == 2 * (dus + i) + 1)(functools.partial(total, i, AXES, own, got, l_send, l_recv))
     pl.when(slot == pl.num_programs(0) - 1)(finish)
 
 

time: 471 us -> 456 us (0.968)
  Pallas kernels: 429 us -> 413 us
    pallas_call x1, Pallas kernels: 84.3 us -> 67.6 us  [stats_call(): pl.pallas_call(stats_kernel, grid=(VSH // SVB,), in_specs=[whole((D, HALF...]
where the time goes in v4:
time: 456 us; the launch traced here: 455 us
  Pallas kernels  413 us (91%)
  local copies, waits for them, and re-layouts  41.2 us (9%)
    pallas_call x1, Pallas kernels, main_call(): pl.pallas_call(main_kernel, grid=(2 * K + 12,), in_specs=[whole((nz, 8, T...  329 us
    pallas_call x1, Pallas kernels, stats_call(): pl.pallas_call(stats_kernel, grid=(VSH // SVB,), in_specs=[whole((D, HALF...  67.6 us
    unnamed x1, local copies, waits for them, and re-layouts  38.5 us

profile of v4, /device:TPU:0, one launch (start us, length us, event | category | flops | bytes accessed | tf_op | source)
XLA Modules:
  0.0 455.3 jit_solution(9179541472464181781)
XLA Ops:
  0.6 1.5 reshape.11.g_ref
  2.2 3.5 norm.1
  5.6 67.6 %stats.1 = (f32[1024,24576]{1,0:T(8,128)}, f32[4,8,1024]{2,1,0:T(8,128)}, f32[2,3,576,512]{3,2,1,0:T(8,128)}) custom-call(f32[576,512]{1,0:T(8,128)} %get-tuple-element.14.pay, s32[2,512]{1,0:T(2,128)} %mask_ref.1, s32[2,512]{1,0:T(2,128)} %lab_ref.1, bf16[1024,576]{1,0:T(8,128)(2,1)} %get-tuple-element.15.u_ref, bf16[576,24576]{1,0:T(8,128)(2,1)} %bitcast.11), custom_call_target="tpu_custom_call" | custom-call | flops 28991029248 | bytes 100663296 | tf_op jit(solution)/shard_map/stats/pallas_call | solution.py:293
  73.3 8.7 %pack.1 = (bf16[4096,576]{1,0:T(8,128)(2,1)}, bf16[576,4096]{1,0:T(8,128)(2,1)}) custom-call(bf16[1024,576]{1,0:T(8,128)(2,1)} %get-tuple-element.15.u_ref, bf16[576,1024]{1,0:T(8,128)(2,1)} %get-tuple-element.17.ut_ref, f32[2,3,576,512]{3,2,1,0:T(8,128)} %get-tuple-element.18.own_ref.sib_ref, f32[2,3,576,512]{3,2,1,0:T(8,128)} %get-tuple-element.18.own_ref.sib_ref), custom_call_target="tpu_custom_call" | custom-call | tf_op jit(solution)/shard_map/pack/pallas_call | solution.py:351
  82.0 329.0 %main.1 = (f32[4,144,24576]{2,1,0:T(8,128)}, f32[2,1024,640]{2,1,0:T(8,128)}, f32[8,128]{1,0:T(8,128)}) custom-call(f32[4,8,1024]{2,1,0:T(8,128)} %get-tuple-element.16.rows_ref, bf16[4096,576]{1,0:T(8,128)(2,1)} %get-tuple-element.19.u_ref, bf16[576,4096]{1,0:T(8,128)(2,1)} %get-tuple-element.20.ut_ref, bf16[576,24576]{1,0:T(8,128)(2,1)} %bitcast.12, ...), custom_call_target="tpu_custom_call" | custom-call | flops 86973087744 | bytes 100663296 | tf_op jit(solution)/shard_map/main/pallas_call | solution.py:624
  411.0 1.2 slice.3
  412.2 4.7 %norm_back.1 = bf16[2,576,512]{2,1,0:T(8,128)(2,1)} custom-call(bf16[2,576,512]{2,1,0:T(8,128)(2,1)} %bitcast.9, f32[576,1]{1,0:T(8,128)} %reshape.11.g_ref, f32[2,1024,640]{2,1,0:T(8,128)} %get-tuple-element.23.du_ref), custom_call_target="tpu_custom_call" | custom-call | tf_op jit(solution)/shard_map/norm_back/pallas_call | solution.py:161
  416.8 38.5 %copy.11 = f32[24576,576]{0,1:T(8,128)} copy(f32[24576,576]{0,1:T(8,128)} %bitcast.7) | data formatting | bytes 113246208
